TPU v7x, 32 devices: a whole 2x2x4 slice. The times are simulated.
32 devices in a mesh: gx: 4 (over z), gy: 4 (over x, core), ens: 2 (over y).
Axes of the slice: x: 2, y: 2, z: 4, core: 2. Of those that a mesh axis runs over, the one named last changes fastest.
Arguments:
- state: float32 [128, 64, 512], P('ens', 'gy', 'gx'), may hold values from -6 to 6
- u_vel: float32 [64, 512], P('gy', 'gx'), may hold values from -0.4 to 0.4
- v_vel: float32 [64, 512], P('gy', 'gx'), may hold values from -0.4 to 0.4
- land: int32 [64, 512], P('gy', 'gx'), may hold values 0 or 1
- forcing: float32 [8, 64, 512], P(None, 'gy', 'gx'), may hold values from -3 to 3
- member_mode: int32 [128], P('ens'), may hold values from 0 to 7
- theta: float32 [128, 4], P('ens'), may hold values from -1 to 1
- obs_index: int32 [4, 4, 128], P('gy', 'gx'), may hold values from 0 to 2047
- obs_values: float32 [4, 4, 128], P('gy', 'gx'), may hold values from -6 to 6
- obs_sigma: float32 [4, 4, 128], P('gy', 'gx'), may hold values from 0.5 to 4
Outputs:
- final_state: float32 [128, 64, 512], P('ens', 'gy', 'gx')
- new_theta: float32 [128, 4], P('ens')
All inputs are finite; a program needn't handle non-finite values. No bound on the sum of `land` on one device may be relied on, other than what follows from the above.
Results may differ from a plain program's by a relative error of at most 0.0003.
Values sent between devices are 32-bit elements; how exact they have to be, the bound alone decides.
A program may use at most 64 MiB of HBM per device.

v0:
```python
import jax
import jax.numpy as jnp
from jax import lax
from jax.sharding import PartitionSpec as P

STEPS = 4


def with_halo(block, sides, width):
    for axis, dim in sides:
        count = lax.axis_size(axis)
        forward = [(i, i + 1) for i in range(count - 1)]
        forward.append((count - 1, 0))
        backward = [(target, source) for source, target in forward]
        low = lax.ppermute(
            lax.slice_in_dim(block, block.shape[dim] - width, None, axis=dim), axis, forward
        )
        high = lax.ppermute(lax.slice_in_dim(block, 0, width, axis=dim), axis, backward)
        block = jnp.concatenate([low, block, high], axis=dim)
    return block


def laplace(field):
    return (
        field[:, 2:, 1:-1]
        + field[:, :-2, 1:-1]
        + field[:, 1:-1, 2:]
        + field[:, 1:-1, :-2]
        - 4.0 * field[:, 1:-1, 1:-1]
    )


def wall_mask(rows_here, width):
    first = lax.axis_index("gy") * rows_here - width
    row_ids = first + jnp.arange(rows_here + 2 * width, dtype=jnp.int32)
    inside = (row_ids >= 0) & (row_ids < rows_here * lax.axis_size("gy"))
    return inside.astype(jnp.float32)[None, :, None]


def cropped(field, margin):
    rows_all = field.shape[-2]
    cols_all = field.shape[-1]
    return field[..., margin : rows_all - margin, margin : cols_all - margin]


def local(state, u_vel, v_vel, land, forcing, member_mode, theta, obs_index, obs_values, obs_sigma):
    members_here, rows_here, cols_here = state.shape
    ocean = (1 - land).astype(jnp.float32)
    diffuse = (0.05 * (1.0 + 0.5 * jnp.tanh(theta[:, 0])))[:, None, None]
    hyper = (0.005 * (1.0 + 0.5 * jnp.tanh(theta[:, 1])))[:, None, None]
    damping = (0.05 * (1.0 + 0.5 * jnp.tanh(theta[:, 2])))[:, None, None]
    patterns = forcing.shape[0]
    one_hot = (member_mode[:, None] == jnp.arange(patterns, dtype=jnp.int32)[None, :]).astype(
        jnp.float32
    )
    picked = jnp.dot(
        one_hot,
        forcing.reshape(patterns, rows_here * cols_here),
        preferred_element_type=jnp.float32,
        precision=lax.Precision.HIGHEST,
    )
    forced = theta[:, 3][:, None, None] * picked.reshape(members_here, rows_here, cols_here)
    depth = 2 * STEPS
    packed = jnp.concatenate([state, forced, u_vel[None], v_vel[None], ocean[None]], 0)
    widened = with_halo(packed, (("gx", 2), ("gy", 1)), depth)
    field_wide = widened[:members_here]
    forced_wide = widened[members_here : 2 * members_here]
    u_wide = widened[2 * members_here]
    v_wide = widened[2 * members_here + 1]
    ocean_wide = widened[2 * members_here + 2]
    for step_index in range(STEPS):
        margin = depth - 2 * step_index
        extended = field_wide * wall_mask(rows_here, margin)
        lap_wide = laplace(extended) * wall_mask(rows_here, margin - 1)
        biharm = laplace(lap_wide)
        lap_field = lap_wide[:, 1:-1, 1:-1]
        center = extended[:, 2:-2, 2:-2]
        grad_x = 0.5 * (extended[:, 2:-2, 3:-1] - extended[:, 2:-2, 1:-3])
        grad_y = 0.5 * (extended[:, 3:-1, 2:-2] - extended[:, 1:-3, 2:-2])
        offset = 2 * step_index + 2
        tend = (
            diffuse * lap_field
            - hyper * biharm
            - damping * center
            + cropped(forced_wide, offset)
            - (cropped(u_wide, offset) * grad_x + cropped(v_wide, offset) * grad_y)
        )
        field_wide = (center + tend) * cropped(ocean_wide, offset)
    site_index = obs_index.reshape(-1)
    observed_here = jnp.take(
        field_wide.reshape(members_here, rows_here * cols_here), site_index, axis=1
    )
    observed, theta_all = (
        lax.all_gather(observed_here, "ens", axis=0, tiled=True),
        lax.all_gather(theta, "ens", axis=0, tiled=True),
    )
    sigma = obs_sigma.reshape(-1)
    target = obs_values.reshape(-1)
    anomaly = (observed - jnp.mean(observed, 0)) / sigma
    misfit = (target - observed) / sigma
    total = observed.shape[0]
    start = lax.axis_index("ens") * members_here
    gram_part = jnp.dot(
        anomaly, anomaly.T, preferred_element_type=jnp.float32, precision=lax.Precision.HIGHEST
    )
    cross_part = jnp.dot(
        anomaly, misfit.T, preferred_element_type=jnp.float32, precision=lax.Precision.HIGHEST
    )
    gram, cross_sum = lax.psum((gram_part, cross_part), ("gx", "gy"))
    cross_own = lax.dynamic_slice_in_dim(cross_sum, start, members_here, 1)
    system = gram + (total - 1) * jnp.eye(total, dtype=jnp.float32)
    factor = jnp.linalg.cholesky(system)
    weights = jax.scipy.linalg.cho_solve((factor, True), cross_own)
    spread = theta_all - jnp.mean(theta_all, 0)
    new_theta = theta + jnp.dot(
        weights.T, spread, preferred_element_type=jnp.float32, precision=lax.Precision.HIGHEST
    )
    return (field_wide, new_theta)


def solution(mesh):
    placed = (
        P("ens", "gy", "gx"),
        P("gy", "gx"),
        P("gy", "gx"),
        P("gy", "gx"),
        P(None, "gy", "gx"),
        P("ens"),
        P("ens", None),
        P("gy", "gx", None),
        P("gy", "gx", None),
        P("gy", "gx", None),
    )
    return jax.shard_map(
        local,
        mesh=mesh,
        in_specs=placed,
        out_specs=(P("ens", "gy", "gx"), P("ens", None)),
        check_vma=False,
    )
```

profile of v0, /device:TPU:0, one launch (start us, length us, event | category | flops | bytes accessed | tf_op | source)
XLA Modules:
  0.0 210.1 jit_solution(9650202040542061370)
XLA Ops:
  7.2 0.8 multiply_bitcast_fusion.2
  8.1 1.2 copy.23
  9.3 0.7 subtract_convert_fusion
  10.0 1.3 convolution_multiply_fusion
  11.3 0.3 concatenate.9
  11.6 1.3 fusion.77
  13.0 1.8 copy.24
  14.8 3.1 %collective-permute-start = (f32[131,16,8]{0,2,1:T(8,128)S(1)}, f32[131,16,8]{0,2,1:T(8,128)S(1)}, u32[]{:S(2)}, u32[]{:S(2)}) collective-permute-start(f32[131,16,8]{0,2,1:T(8,128)S(1)} %copy.24), channel_id=1, source_target_pairs={{0,8},{8,16},{16,24},{24,0},{1,9},{9,17},{17,25},{25,1},{2,10},{10... | collective-permute-start | bytes 201224 | tf_op jit(solution)/shard_map/ppermute | solution.py:15
  17.8 0.6 copy.25
  18.4 2.1 collective-permute-start.1
  20.6 3.5 %collective-permute-done = f32[131,16,8]{0,2,1:T(8,128)S(1)} collective-permute-done((f32[131,16,8]{0,2,1:T(8,128)S(1)}, f32[131,16,8]{0,2,1:T(8,128)S(1)}, u32[]{:S(2)}, u32[]{:S(2)}) %collective-permute-start) | collective-permute-done | bytes 67104 | tf_op jit(solution)/shard_map/ppermute | solution.py:15
  24.1 0.4 copy.26
  24.5 1.7 collective-permute-done.1
  26.2 0.4 copy.27
  26.5 0.9 pad_maximum_fusion.1
  27.5 0.2 fusion.76
  27.6 1.3 copy.28
  29.0 1.3 copy.29
  30.3 1.7 collective-permute-start.3
  32.0 4.4 %all-gather = f32[2,64,4]{1,2,0:T(4,128)S(1)} all-gather(f32[1,64,4]{1,2,0:T(4,128)S(1)} %bitcast.66), channel_id=1, replica_groups=mesh['gx'=4,'gy'=4,'ens'=2] {'ens'}, dimensions={0}, use_global_device_ids=true | all-gather | bytes 3072 | tf_op jit(solution)/shard_map/all_gather | solution.py:95
  36.4 0.1 reduce_sum.19
  36.5 15.6 %collective-permute-done.2 = f32[131,8,144]{2,1,0:T(8,128)} collective-permute-done((f32[131,8,144]{2,1,0:T(8,128)}, f32[131,8,144]{2,1,0:T(8,128)}, u32[]{:S(2)}, u32[]{:S(2)}) %collective-permute-start.2) | collective-permute-done | bytes 603680 | tf_op jit(solution)/shard_map/ppermute | solution.py:15
  52.2 1.6 copy.30
  53.8 0.5 collective-permute-done.3
  54.3 1.6 copy.31
  55.9 0.2 pad_maximum_fusion.4
  56.1 1.0 pad_maximum_fusion
  57.1 0.1 slice.403
  57.2 0.1 slice.422
  57.3 0.1 slice_multiply_fusion.6
  57.4 0.1 slice_multiply_fusion.10
  57.5 0.1 slice_multiply_fusion.5
  57.5 0.1 slice_multiply_fusion.9
  57.6 0.1 slice.441
  57.7 0.1 slice_multiply_fusion.8
  57.8 0.1 slice_multiply_fusion.7
  58.1 0.2 slice_multiply_fusion
  58.3 2.1 %fusion.1 = f32[64,30,142]{2,0,1:T(8,128)S(1)} fusion(f32[64,32,144]{2,0,1:T(8,128)S(1)} %slice_multiply_fusion, f32[30]{0:T(128)S(1)} %and_convert_fusion.6), kind=kLoop, calls=%fused_computation.6 | loop fusion | flops 1635840 | bytes 6543480 | tf_op jit(solution)/shard_map/mul | solution.py:74
  60.4 5.3 %fusion.7 = f32[64,28,140]{2,0,1:T(8,128)S(1)} fusion(f32[64,32,144]{2,0,1:T(8,128)S(1)} %slice_multiply_fusion, f32[131,32,144]{2,0,1:T(8,128)S(1)} %pad_maximum_fusion, f32[64,30,142]{2,0,1:T(8,128)S(1)} %fusion.1, f32[28]{0:T(128)S(1)} %and_convert_fusion.5, f32[28,140]{1,0:T(8,128)S(1)} %slice.403, f32[28,140]{1,0:T(8,128)S(1)} %slice_multiply_fusion.5, ...), kind=kLoop, calls=%fused_computation.16 | loop fusion | flops 5017600 | bytes 12090160 | tf_op jit(solution)/shard_map/mul | solution.py:73
  65.7 1.8 fusion.14
  67.5 4.4 %fusion.20 = f32[64,24,136]{2,0,1:T(8,128)S(1)} fusion(f32[64,28,140]{2,0,1:T(8,128)S(1)} %fusion.7, f32[131,32,144]{2,0,1:T(8,128)S(1)} %pad_maximum_fusion, f32[64,26,138]{2,0,1:T(8,128)S(1)} %fusion.14, f32[24]{0:T(128)S(1)} %and_convert_fusion.3, f32[24,136]{1,0:T(8,128)S(1)} %slice.422, f32[24,136]{1,0:T(8,128)S(1)} %slice_multiply_fusion.9, ...), kind=kLoop, calls=%fused_computation.39 | loop fusion | flops 4177920 | bytes 10067040 | tf_op jit(solution)/shard_map/mul | solution.py:73
  72.0 1.6 fusion.27
  73.6 3.7 %fusion.33 = f32[64,20,132]{2,0,1:T(8,128)S(1)} fusion(f32[64,24,136]{2,0,1:T(8,128)S(1)} %fusion.20, f32[131,32,144]{2,0,1:T(8,128)S(1)} %pad_maximum_fusion, f32[64,22,134]{2,0,1:T(8,128)S(1)} %fusion.27, f32[20]{0:T(128)S(1)} %and_convert_fusion.1, f32[20,132]{1,0:T(8,128)S(1)} %slice.441, f32[20,132]{1,0:T(8,128)S(1)} %slice_multiply_fusion.7, ...), kind=kLoop, calls=%fused_computation.62 | loop fusion | flops 3379200 | bytes 8142608 | tf_op jit(solution)/shard_map/mul | solution.py:73
  77.3 1.3 fusion.40
  78.6 1.3 fusion.45
  80.0 0.3 copy.39
  80.3 0.6 gather_fusion
  80.9 0.1 select_bitcast_fusion
  81.1 5.0 %all_gather.6 = f32[128,128]{1,0:T(8,128)S(1)} all-gather(f32[64,128]{1,0:T(8,128)S(1)} %copy.35), channel_id=1, replica_groups=mesh['gx'=4,'gy'=4,'ens'=2] {'ens'}, dimensions={0}, use_global_device_ids=true | all-gather | bytes 98304 | tf_op jit(solution)/shard_map/all_gather | solution.py:94
  86.1 0.9 fusion.62
  87.0 0.9 fusion.59
  88.0 0.1 reshape.208
  88.1 1.1 copy.38
  89.2 87.4 %all-reduce.3.cloned.1.call-done = (f32[128,128]{1,0:T(8,128)}, f32[128,128]{0,1:T(8,128)}) async-done(((f32[128,128]{1,0:T(8,128)}, f32[128,128]{0,1:T(8,128)}), (f32[128,128]{1,0:T(8,128)}, f32[128,128]{0,1:T(8,128)})) %all-reduce.3.cloned.1.call-update) | async-done | bytes 131088 | tf_op jit(solution)/shard_map/psum | solution.py:109
  176.6 0.9 select_add_fusion
  177.4 0.1 copy.36
  177.5 0.9 fusion.58
  178.4 11.7 %cholesky.16 = f32[128,128]{1,0:T(8,128)S(1)} custom-call(f32[128,128]{1,0:T(8,128)S(1)} %fusion.58), custom_call_target="Cholesky" | custom-call | tf_op jit(solution)/shard_map/jit(cholesky)/cholesky | solution.py:112
  190.1 0.6 compare_reduce_fusion
  190.8 0.7 fusion.52
  191.4 9.8 %custom-call.10 = f32[1,128,128]{1,2,0:T(8,128)S(1)} custom-call(f32[1,128,128]{2,1,0:T(8,128)S(1)} %fusion.52), custom_call_target="InvertDiagBlocksLowerTriangular" | custom-call | tf_op jit(solution)/shard_map/jit(_cho_solve)/triangular_solve | solution.py:113
  201.3 0.9 fusion.56
  202.2 0.2 fusion.54
  202.5 0.8 convolution_add_fusion
  (41 shorter events, 0.5 us)
Async XLA Ops:
  7.2 4.1 %copy-start.2 = (f32[16,128]{1,0:T(8,128)S(1)}, f32[16,128]{1,0:T(8,128)}, u32[]{:S(2)}) copy-start(f32[16,128]{1,0:T(8,128)} %param.11) | copy-start | bytes 24580
  7.2 4.1 %copy-start.3 = (f32[16,128]{1,0:T(8,128)S(1)}, f32[16,128]{1,0:T(8,128)}, u32[]{:S(2)}) copy-start(f32[16,128]{1,0:T(8,128)} %param.12) | copy-start | bytes 24580
  7.2 169.4 %all-reduce.3.cloned.1.call-start = ((), (), s32[]{:S(2)}) async-start(), calls=%async_computation | async-start | bytes 262144 | tf_op jit(solution)/shard_map/psum | solution.py:109
  11.3 1.7 copy-start
  14.8 9.4 %collective-permute-start = (f32[131,16,8]{0,2,1:T(8,128)S(1)}, f32[131,16,8]{0,2,1:T(8,128)S(1)}, u32[]{:S(2)}, u32[]{:S(2)}) collective-permute-start(f32[131,16,8]{0,2,1:T(8,128)S(1)} %copy.24), channel_id=1, source_target_pairs={{0,8},{8,16},{16,24},{24,0},{1,9},{9,17},{17,25},{25,1},{2,10},{10... | collective-permute-start | bytes 201224 | tf_op jit(solution)/shard_map/ppermute | solution.py:15
  18.4 7.8 %collective-permute-start.1 = (f32[131,16,8]{0,2,1:T(8,128)S(1)}, f32[131,16,8]{0,2,1:T(8,128)S(1)}, u32[]{:S(2)}, u32[]{:S(2)}) collective-permute-start(f32[131,16,8]{0,2,1:T(8,128)S(1)} %copy.25), channel_id=1, source_target_pairs={{8,0},{16,8},{24,16},{0,24},{9,1},{17,9},{25,17},{1,25},{10,2},{18... | collective-permute-start | bytes 201224 | tf_op jit(solution)/shard_map/ppermute | solution.py:18
  29.0 3.1 %copy-start.4 = (f32[64,4]{0,1:T(4,128)S(1)}, f32[64,4]{0,1:T(4,128)}, u32[]{:S(2)}) copy-start(f32[64,4]{0,1:T(4,128)} %param.16) | copy-start | bytes 3076
  29.0 7.5 %copy-start.5 = (s32[1,1,128]{2,1,0:T(1,128)S(1)}, s32[1,1,128]{2,1,0:T(1,128)}, u32[]{:S(2)}) copy-start(s32[1,1,128]{2,1,0:T(1,128)} %param.17) | copy-start | bytes 1540
  29.0 23.2 %collective-permute-start.2 = (f32[131,8,144]{2,1,0:T(8,128)}, f32[131,8,144]{2,1,0:T(8,128)}, u32[]{:S(2)}, u32[]{:S(2)}) collective-permute-start(f32[131,8,144]{2,1,0:T(8,128)} %copy.28), channel_id=1, source_target_pairs={{0,2},{2,4},{4,6},{6,0},{1,3},{3,5},{5,7},{7,1},{8,10},{10,12},{12... | collective-permute-start | bytes 1810952 | tf_op jit(solution)/shard_map/ppermute | solution.py:15
  30.3 24.0 %collective-permute-start.3 = (f32[131,8,144]{2,1,0:T(8,128)}, f32[131,8,144]{2,1,0:T(8,128)}, u32[]{:S(2)}, u32[]{:S(2)}) collective-permute-start(f32[131,8,144]{2,1,0:T(8,128)} %copy.29), channel_id=1, source_target_pairs={{2,0},{4,2},{6,4},{0,6},{3,1},{5,3},{7,5},{1,7},{10,8},{12,10},{14... | collective-permute-start | bytes 1810952 | tf_op jit(solution)/shard_map/ppermute | solution.py:18
  77.3 1.3 copy-start.1
  79.9 6.2 %copy-start.6 = (f32[1,1,128]{2,1,0:T(1,128)S(1)}, f32[1,1,128]{2,1,0:T(1,128)}, u32[]{:S(2)}) copy-start(f32[1,1,128]{2,1,0:T(1,128)} %param.19) | copy-start | bytes 1540
  79.9 7.1 %copy-start.7 = (f32[1,1,128]{2,1,0:T(1,128)S(1)}, f32[1,1,128]{2,1,0:T(1,128)}, u32[]{:S(2)}) copy-start(f32[1,1,128]{2,1,0:T(1,128)} %param.18) | copy-start | bytes 1540
Sparse Core Ops, SparseCore 0:
  88.1 88.4 all-reduce.2
where the time goes:
time: 212 us; the launch traced here: 210 us
  waiting for transfers between devices  109 us (51%)
  other arithmetic  51 us (24%)
  local copies, waits for them, and re-layouts  14.6 us (7%)
  between operations  14.4 us (7%)
  blocking collectives  9.36 us (4%)
  starting transfers between devices  6.93 us (3%)
  matrix products  5.06 us (2%)
    psum x1, waiting for transfers between devices, local(): gram, cross_sum = lax.psum((gram_part, cross_part), ('gx', 'gy'))  87.4 us
    ppermute x2, waiting for transfers between devices, with_halo(): lax.ppermute(lax.slice_in_dim(block, block.shape[dim] - width, None, axis...  19.2 us
    mul x4, other arithmetic, local(): extended = field_wide * wall_mask(rows_here, margin)  13.6 us
    another operation x3, other arithmetic, local(): factor = jnp.linalg.cholesky(system)  12.4 us
    another operation x2, other arithmetic, local(): weights = jax.scipy.linalg.cho_solve((factor, True), cross_own)  10.5 us
    mul x4, other arithmetic, local(): lap_wide = laplace(extended) * wall_mask(rows_here, margin - 1)  6.85 us
    all_gather x1, blocking collectives, local(): lax.all_gather(observed_here, 'ens', axis=0, tiled=True)  5 us
    slice x4, local copies, waits for them, and re-layouts, with_halo(): lax.slice_in_dim(block, block.shape[dim] - width, None, axis=dim)  4.63 us
  transfers between devices with their start and end apart: 5, of which 5 were waited for; matrix products, arithmetic and copies ran while one was open for 2% of the time, Pallas kernels for 0%

commit v1 on v0

v1 whole, which is shorter than its diff:
```python
import functools
import jax
import jax.numpy as jnp
from jax import lax
from jax.experimental import pallas as pl
from jax.experimental.pallas import tpu as pltpu
from jax.sharding import PartitionSpec as P

STEPS = 4
DEPTH = 2 * STEPS
F32 = jnp.float32
VM = pltpu.VMEM
MESH = pl.DeviceIdType.MESH
HIGH = lax.Precision.HIGHEST


def vspec():
    return pl.BlockSpec(memory_space=pltpu.VMEM)


def halo_kernel(n_gx, n_gy, q_ref, f_ref, qt_ref, qb_ref, ft_ref, fb_ref, mid_ref, top_ref, bot_ref,
                pack, row_send, row_recv, gx_send, gx_recv, gy_send, gy_recv):
    gx, gy = lax.axis_index("gx"), lax.axis_index("gy")
    right, left = lax.rem(gx + 1, n_gx), lax.rem(gx + n_gx - 1, n_gx)
    has_up, has_down = gy > 0, gy < n_gy - 1
    up, down = jnp.maximum(gy - 1, 0), jnp.minimum(gy + 1, n_gy - 1)
    members, rows, cols = q_ref.shape
    fields = f_ref.shape[0]

    barrier = pltpu.get_barrier_semaphore()
    pl.semaphore_signal(barrier, inc=1, device_id={"gx": right}, device_id_type=MESH)
    pl.semaphore_signal(barrier, inc=1, device_id={"gx": left}, device_id_type=MESH)

    @pl.when(has_up)
    def _():
        pl.semaphore_signal(barrier, inc=1, device_id={"gy": up}, device_id_type=MESH)

    @pl.when(has_down)
    def _():
        pl.semaphore_signal(barrier, inc=1, device_id={"gy": down}, device_id_type=MESH)

    lane = lax.broadcasted_iota(jnp.int32, (8, cols), 1)

    def pack_from(ref, base):
        def body(g, carry):
            lo = jnp.zeros((8, cols), F32)
            hi = jnp.zeros((8, cols), F32)
            for r in range(rows):
                val = ref[pl.ds(g * 8, 8), r, :]
                mine = (lane // DEPTH) == r
                hi = jnp.where(mine, pltpu.roll(val, (r * DEPTH + DEPTH) % cols, 1), hi)
                lo = jnp.where(mine, pltpu.roll(val, (r * DEPTH) % cols, 1), lo)
            pack[0, pl.ds(base + g * 8, 8), :] = hi
            pack[1, pl.ds(base + g * 8, 8), :] = lo
            return carry
        lax.fori_loop(0, ref.shape[0] // 8, body, 0)

    pl.semaphore_wait(barrier, 2 + has_up.astype(jnp.int32) + has_down.astype(jnp.int32))

    def rdma(src, dst, send, recv, dev):
        return pltpu.make_async_remote_copy(src_ref=src, dst_ref=dst, send_sem=send, recv_sem=recv,
                                            device_id=dev, device_id_type=MESH)

    downs = [rdma(q_ref.at[:, rows - DEPTH:, :], qt_ref, row_send.at[0], row_recv.at[0], {"gy": down}),
             rdma(f_ref.at[:, rows - DEPTH:, :], ft_ref, row_send.at[1], row_recv.at[1], {"gy": down})]
    ups = [rdma(q_ref.at[:, :DEPTH, :], qb_ref, row_send.at[2], row_recv.at[2], {"gy": up}),
           rdma(f_ref.at[:, :DEPTH, :], fb_ref, row_send.at[3], row_recv.at[3], {"gy": up})]
    strip_down = rdma(mid_ref, top_ref, gy_send.at[0], gy_recv.at[0], {"gy": down})
    strip_up = rdma(mid_ref, bot_ref, gy_send.at[1], gy_recv.at[1], {"gy": up})

    @pl.when(has_down)
    def _():
        for c in downs:
            c.start()

    @pl.when(has_up)
    def _():
        for c in ups:
            c.start()

    pack_from(q_ref, 0)
    pack_from(f_ref, members)
    to_right = rdma(pack.at[0], mid_ref.at[0], gx_send.at[0], gx_recv.at[0], {"gx": right})
    to_left = rdma(pack.at[1], mid_ref.at[1], gx_send.at[1], gx_recv.at[1], {"gx": left})
    to_right.start()
    to_left.start()
    to_right.wait()
    to_left.wait()

    @pl.when(has_down)
    def _():
        strip_down.start()

    @pl.when(has_up)
    def _():
        strip_up.start()

    @pl.when(has_down)
    def _():
        for c in downs + [strip_down]:
            c.wait_send()
        for c in ups + [strip_up]:
            c.wait_recv()

    @pl.when(has_up)
    def _():
        for c in ups + [strip_up]:
            c.wait_send()
        for c in downs + [strip_down]:
            c.wait_recv()


def halo_exchange(mesh, state, fields):
    members, rows, cols = state.shape
    nf = fields.shape[0]
    total = members + nf
    sds = jax.ShapeDtypeStruct
    return pl.pallas_call(
        functools.partial(halo_kernel, mesh.shape["gx"], mesh.shape["gy"]),
        out_shape=[sds((members, DEPTH, cols), F32), sds((members, DEPTH, cols), F32),
                   sds((nf, DEPTH, cols), F32), sds((nf, DEPTH, cols), F32),
                   sds((2, total, cols), F32), sds((2, total, cols), F32), sds((2, total, cols), F32)],
        in_specs=[vspec()] * 2,
        out_specs=[vspec()] * 7,
        scratch_shapes=[VM((2, total, cols), F32)]
        + [pltpu.SemaphoreType.DMA((4,))] * 2
        + [pltpu.SemaphoreType.DMA((2,))] * 4,
        compiler_params=pltpu.CompilerParams(collective_id=0, has_side_effects=True),
        name="halo",
    )(state, fields)


def model_kernel(n_gy, rows, q_ref, qt_ref, qb_ref, mid_ref, top_ref, bot_ref,
                 f_ref, ft_ref, fb_ref, fmid_ref, ftop_ref, fbot_ref,
                 mode_ref, theta_ref, index_ref, out_ref, obs_ref, thp_ref,
                 Q, FO, FP, ST):
    g = pl.program_id(0)
    gy = lax.axis_index("gy")
    cols = 128
    has_up, has_down = gy > 0, gy < n_gy - 1
    n_rows = rows + 2 * DEPTH
    shape = (8, cols)
    lane = lax.broadcasted_iota(jnp.int32, shape, 1)
    sub = lax.broadcasted_iota(jnp.int32, shape, 0)
    zero = jnp.zeros(shape, F32)

    def inside(i):
        return has_up if i < DEPTH else (has_down if i >= DEPTH + rows else None)

    def masked(i, x):
        ok = inside(i)
        return x if ok is None else jnp.where(ok, x, 0.0)

    def row_pair(i, base, q, qt, qb, mid, top, bot, mbase):
        if i < DEPTH:
            a = qt[pl.ds(base * DEPTH + i, 8, stride=DEPTH), :]
            strip, k = top, rows - DEPTH + i
        elif i < DEPTH + rows:
            a = q[pl.ds(base * rows + i - DEPTH, 8, stride=rows), :]
            strip, k = mid, i - DEPTH
        else:
            a = qb[pl.ds(base * DEPTH + i - DEPTH - rows, 8, stride=DEPTH), :]
            strip, k = bot, i - DEPTH - rows
        lo = pltpu.roll(strip[0, mbase:mbase + 8, :], (cols - DEPTH - k * DEPTH) % cols, 1)
        hi = pltpu.roll(strip[1, mbase:mbase + 8, :], (cols - k * DEPTH) % cols, 1)
        b = jnp.where(lane < DEPTH, hi, jnp.where(lane >= cols - DEPTH, lo, 0.0))
        return masked(i, a), masked(i, b)

    @pl.when(g == 0)
    def _():
        for i in range(n_rows):
            pa, pb = row_pair(i, 0, f_ref, ft_ref, fb_ref, fmid_ref, ftop_ref, fbot_ref, 0)
            FP[i, 0] = pa
            FP[i, 1] = pb
            sa, sb = row_pair(i, 8, f_ref, ft_ref, fb_ref, fmid_ref, ftop_ref, fbot_ref, 8)
            for h, s in ((0, sa), (1, sb)):
                ST[0, i, h] = jnp.broadcast_to(0.5 * s[0:1], shape)
                ST[1, i, h] = jnp.broadcast_to(0.5 * s[1:2], shape)
                ST[2, i, h] = jnp.broadcast_to(s[2:3], shape)

    th = theta_ref[...]
    diffuse = jnp.broadcast_to(0.05 * (1.0 + 0.5 * jnp.tanh(th[:, 0:1])), shape)
    hyper = jnp.broadcast_to(0.005 * (1.0 + 0.5 * jnp.tanh(th[:, 1:2])), shape)
    keep = jnp.broadcast_to(1.0 - 0.05 * (1.0 + 0.5 * jnp.tanh(th[:, 2:3])), shape)
    gain = jnp.broadcast_to(th[:, 3:4], shape)
    thp = zero
    for k in range(th.shape[1]):
        thp = jnp.where(lane == k, th[:, k:k + 1], thp)
    thp_ref[...] = thp

    mode = jnp.zeros(shape, jnp.int32)
    for k in range(8):
        mode = jnp.where(sub == k, mode_ref[g * 8 + k], mode)

    for i in range(n_rows):
        a, b = row_pair(i, 0, q_ref, qt_ref, qb_ref, mid_ref, top_ref, bot_ref, 0)
        Q[0, i, 0] = a
        Q[0, i, 1] = b
        if 2 <= i < n_rows - 2:
            for h in range(2):
                FO[i, h] = gain * jnp.take_along_axis(FP[i, h], mode, axis=0, mode="promise_in_bounds")

    first, last = lane == 0, lane == cols - 1

    def neighbours(a, b):
        ap, bp = pltpu.roll(a, cols - 1, 1), pltpu.roll(b, cols - 1, 1)
        am, bm = pltpu.roll(a, 1, 1), pltpu.roll(b, 1, 1)
        return ((jnp.where(last, bp, ap), jnp.where(first, bm, am)),
                (jnp.where(last, ap, bp), jnp.where(first, am, bm)))

    for s in range(STEPS):
        src, dst = s % 2, (s + 1) % 2
        lo, hi = 2 * s, n_rows - 2 * s
        final = s == STEPS - 1
        q, lap, grad = {}, {}, {}

        def load(i):
            q[i] = (Q[src, i, 0], Q[src, i, 1])

        def make_lap(i):
            pair = neighbours(*q[i])
            both, gr = [], []
            for h in range(2):
                xp, xm = pair[h]
                v = (q[i + 1][h] + q[i - 1][h]) + (xp + xm) - 4.0 * q[i][h]
                both.append(masked(i, v))
                gr.append(xp - xm)
            lap[i], grad[i] = tuple(both), gr

        load(lo)
        load(lo + 1)
        for i in range(lo + 2, lo + 4):
            load(i)
            make_lap(i - 1)
        for i in range(lo + 2, hi - 2):
            load(i + 2) if i + 2 < hi else None
            make_lap(i + 1)
            pair = neighbours(*lap[i])
            for h in range(1 if final else 2):
                xp, xm = pair[h]
                bi = (lap[i + 1][h] + lap[i - 1][h]) + (xp + xm) - 4.0 * lap[i][h]
                adv = ST[0, i, h] * grad[i][h] + ST[1, i, h] * (q[i + 1][h] - q[i - 1][h])
                new = keep * q[i][h] + diffuse * lap[i][h] - hyper * bi + (FO[i, h] - adv)
                new = new * ST[2, i, h]
                if final:
                    out_ref[pl.ds(i - DEPTH, 8, stride=rows), :] = new
                else:
                    Q[dst, i, h] = new

    index = index_ref[0]
    col = jnp.bitwise_and(index, cols - 1)
    row = jnp.right_shift(index, cols.bit_length() - 1)
    hot = (lax.broadcasted_iota(jnp.int32, (cols, cols), 0) == col).astype(jnp.bfloat16)
    x = out_ref[...]
    x1 = x.astype(jnp.bfloat16)
    rem = x - x1.astype(F32)
    x2 = rem.astype(jnp.bfloat16)
    x3 = (rem - x2.astype(F32)).astype(jnp.bfloat16)
    dot = functools.partial(jnp.dot, preferred_element_type=F32)
    picked = dot(x1, hot) + (dot(x2, hot) + dot(x3, hot))
    row_id = lax.broadcasted_iota(jnp.int32, (8, rows, cols), 1)
    obs_ref[...] = jnp.sum(jnp.where(row_id == row[None], picked.reshape(8, rows, cols), 0.0), axis=1)


def run_model(mesh, state, fields, halos, member_mode, theta, obs_index):
    members, rows, cols = state.shape
    nf = fields.shape[0]
    qt, qb, ft, fb, mid, top, bot = halos
    n_rows = rows + 2 * DEPTH
    sds = jax.ShapeDtypeStruct
    by_group = lambda n: pl.BlockSpec((8 * n, cols), lambda g: (g, 0))
    strip = pl.BlockSpec((2, 8, cols), lambda g: (0, g, 0))
    fstrip = pl.BlockSpec((2, nf, cols), lambda g: (0, members // nf, 0))
    whole = lambda n: pl.BlockSpec((nf * n, cols), lambda g: (0, 0))
    out, obs, thp = pl.pallas_call(
        functools.partial(model_kernel, mesh.shape["gy"], rows),
        grid=(members // 8,),
        out_shape=[sds((members * rows, cols), F32), sds((members, cols), F32), sds((members, cols), F32)],
        in_specs=[by_group(rows), by_group(DEPTH), by_group(DEPTH), strip, strip, strip,
                  whole(rows), whole(DEPTH), whole(DEPTH), fstrip, fstrip, fstrip,
                  pl.BlockSpec(memory_space=pltpu.SMEM),
                  pl.BlockSpec((8, theta.shape[1]), lambda g: (g, 0)),
                  pl.BlockSpec((1, 1, obs_index.shape[-1]), lambda g: (0, 0, 0))],
        out_specs=[by_group(rows), pl.BlockSpec((8, cols), lambda g: (g, 0)),
                   pl.BlockSpec((8, cols), lambda g: (g, 0))],
        scratch_shapes=[VM((2, n_rows, 2, 8, cols), F32), VM((n_rows, 2, 8, cols), F32),
                        VM((n_rows, 2, 8, cols), F32), VM((3, n_rows, 2, 8, cols), F32)],
        name="model",
    )(state.reshape(members * rows, cols), qt.reshape(-1, cols), qb.reshape(-1, cols), mid, top, bot,
      fields.reshape(-1, cols), ft.reshape(-1, cols), fb.reshape(-1, cols), mid, top, bot,
      member_mode, theta, obs_index)
    return out.reshape(members, rows, cols), obs, thp


def sums_kernel(n_gx, n_gy, n_ens, reduce_here, obs_ref, thp_ref, val_ref, sig_ref, full_ref, th_ref,
                obs_all, part, rs, ens_send, ens_recv, rs_send, rs_recv, ag_send, ag_recv):
    gx, gy, ens = lax.axis_index("gx"), lax.axis_index("gy"), lax.axis_index("ens")
    members = obs_ref.shape[0]
    n = n_gx * n_gy
    me = gy * n_gx + gx
    peers = [lax.rem(me + o, n) for o in range(1, n)] if reduce_here else []
    where = [{"gx": lax.rem(p, n_gx), "gy": lax.div(p, n_gx)} for p in peers]
    others = [lax.rem(ens + o, n_ens) for o in range(1, n_ens)]

    barrier = pltpu.get_barrier_semaphore()
    for p in others:
        pl.semaphore_signal(barrier, inc=1, device_id={"ens": p}, device_id_type=MESH)
    for p in where:
        pl.semaphore_signal(barrier, inc=1, device_id=p, device_id_type=MESH)
    pl.semaphore_wait(barrier, len(others) + len(where))

    def rdma(src, dst, send, recv, dev):
        return pltpu.make_async_remote_copy(src_ref=src, dst_ref=dst, send_sem=send, recv_sem=recv,
                                            device_id=dev, device_id_type=MESH)

    mine = pl.ds(pl.multiple_of(ens * members, members), members)
    copies = []
    for k, p in enumerate(others):
        copies.append(rdma(obs_ref, obs_all.at[mine], ens_send.at[2 * k], ens_recv.at[2 * k], {"ens": p}))
        copies.append(rdma(thp_ref, th_ref.at[mine], ens_send.at[2 * k + 1], ens_recv.at[2 * k + 1], {"ens": p}))
    for c in copies:
        c.start()
    obs_all[mine, :] = obs_ref[...]
    th_ref[mine, :] = thp_ref[...]
    for c in copies:
        c.wait()

    x = obs_all[...]
    mean = jnp.mean(x, axis=0, keepdims=True)
    inv = 1.0 / sig_ref[0]
    anom = (x - mean) * inv
    d = jnp.broadcast_to((val_ref[0] - mean) * inv, x.shape)
    nt = (((1,), (1,)), ((), ()))
    total = x.shape[0]
    part[:, 0:total] = lax.dot_general(anom, anom, nt, preferred_element_type=F32, precision=HIGH)
    part[:, total:] = lax.dot_general(anom, d, nt, preferred_element_type=F32, precision=HIGH)

    if not reduce_here:
        full_ref[...] = part[...]
        return
    own = total // n
    at = lambda p: pl.ds(pl.multiple_of(p * own, own), own)
    sends = [rdma(part.at[at(p)], rs.at[k], rs_send.at[k], rs_recv.at[k], w)
             for k, (p, w) in enumerate(zip(peers, where))]
    for c in sends:
        c.start()
    acc = part[at(me), :]
    for k, c in enumerate(sends):
        c.wait_recv()
        acc = acc + rs[k]
    full_ref[at(me), :] = acc
    gathers = [rdma(full_ref.at[at(me)], full_ref.at[at(me)], ag_send.at[k], ag_recv.at[k], w)
               for k, w in enumerate(where)]
    for c in gathers:
        c.start()
    for c in sends:
        c.wait_send()
    for c in gathers:
        c.wait()


def ensemble_sums(mesh, obs, thp, values, sigma):
    n_gx, n_gy, n_ens = mesh.shape["gx"], mesh.shape["gy"], mesh.shape["ens"]
    members, cols = obs.shape
    total = members * n_ens
    n = n_gx * n_gy
    reduce_here = total % (8 * n) == 0
    own = total // n if reduce_here else 8
    slots = n - 1 if reduce_here else 1
    full, th = pl.pallas_call(
        functools.partial(sums_kernel, n_gx, n_gy, n_ens, reduce_here),
        out_shape=[jax.ShapeDtypeStruct((total, 2 * total), F32), jax.ShapeDtypeStruct((total, cols), F32)],
        in_specs=[vspec()] * 4,
        out_specs=[vspec()] * 2,
        scratch_shapes=[VM((total, cols), F32), VM((total, 2 * total), F32), VM((slots, own, 2 * total), F32)]
        + [pltpu.SemaphoreType.DMA((2 * (n_ens - 1),))] * 2
        + [pltpu.SemaphoreType.DMA((slots,))] * 4,
        compiler_params=pltpu.CompilerParams(collective_id=1, has_side_effects=True),
        name="sums",
    )(obs, thp, values, sigma)
    if not reduce_here:
        full = lax.psum(full, ("gx", "gy"))
    return full, th


def solve_kernel(members, full_ref, th_ref, out_ref, xs):
    total = full_ref.shape[0]
    blocks = total // 8
    shape = (8, total)
    lane = lax.broadcasted_iota(jnp.int32, shape, 1)
    sub = lax.broadcasted_iota(jnp.int32, shape, 0)
    th = th_ref[...]
    mean = jnp.mean(th, axis=0, keepdims=True)
    A, R = [], []
    for k in range(blocks):
        rows = slice(8 * k, 8 * k + 8)
        A.append(full_ref[rows, 0:total] + jnp.where(lane == sub + 8 * k, float(total - 1), 0.0))
        R.append(th[rows] - mean)
    for k in range(blocks):
        pa, pr = A[k], R[k]
        for j in range(8):
            c = pa[:, 8 * k + j:8 * k + j + 1]
            inv = 1.0 / c[j:j + 1]
            na, nr = pa[j:j + 1] * inv, pr[j:j + 1] * inv
            pa = jnp.where(sub == j, na, pa - c * na)
            pr = jnp.where(sub == j, nr, pr - c * nr)
        A[k], R[k] = pa, pr
        for i in list(range(k + 1, blocks)) + list(range(k)):
            a, r = A[i], R[i]
            for j in range(8):
                c = A[i][:, 8 * k + j:8 * k + j + 1]
                a = a - c * pa[j:j + 1]
                r = r - c * pr[j:j + 1]
            A[i], R[i] = a, r
    shift = jnp.zeros((1, th.shape[1]), F32)
    for k in range(blocks):
        rows = slice(8 * k, 8 * k + 8)
        shift = shift + jnp.sum(full_ref[rows, total:] * R[k], axis=0, keepdims=True)
        xs[rows, :] = R[k]
    ens = lax.axis_index("ens")
    x = xs[pl.ds(pl.multiple_of(ens * members, members), members), :]
    new = mean + shift + float(total - 1) * x
    out_ref[...] = new[:, 0:out_ref.shape[1]]


def solve(full, th, theta):
    return pl.pallas_call(
        functools.partial(solve_kernel, theta.shape[0]),
        out_shape=jax.ShapeDtypeStruct(theta.shape, F32),
        in_specs=[vspec()] * 2,
        out_specs=vspec(),
        scratch_shapes=[VM(th.shape, F32)],
        name="solve",
    )(full, th)


def local(mesh, state, u_vel, v_vel, land, forcing, member_mode, theta, obs_index, obs_values, obs_sigma):
    ocean = (1 - land).astype(F32)
    rows, cols = u_vel.shape
    fields = jnp.concatenate([forcing, u_vel[None], v_vel[None], ocean[None], jnp.zeros((5, rows, cols), F32)], 0)
    halos = halo_exchange(mesh, state, fields)
    final, obs, thp = run_model(mesh, state, fields, halos, member_mode, theta, obs_index)
    full, th = ensemble_sums(mesh, obs, thp, obs_values, obs_sigma)
    return final, solve(full, th, theta)


def solution(mesh):
    placed = (
        P("ens", "gy", "gx"),
        P("gy", "gx"),
        P("gy", "gx"),
        P("gy", "gx"),
        P(None, "gy", "gx"),
        P("ens"),
        P("ens", None),
        P("gy", "gx", None),
        P("gy", "gx", None),
        P("gy", "gx", None),
    )
    return jax.shard_map(
        functools.partial(local, mesh),
        mesh=mesh,
        in_specs=placed,
        out_specs=(P("ens", "gy", "gx"), P("ens", None)),
        check_vma=False,
    )
```

time: 212 us -> 75.3 us (0.36)
  waiting for transfers between devices: 109 us -> 0 us
  Pallas kernels: 0 us -> 68.4 us
  other arithmetic: 51 us -> 0.01 us
  between operations: 14.4 us -> 0.67 us
  blocking collectives: 9.36 us -> 0 us
  local copies, waits for them, and re-layouts: 14.6 us -> 5.68 us
  starting transfers between devices: 6.93 us -> 0 us
  matrix products: 5.06 us -> 0 us
    psum x1 -> x0, waiting for transfers between devices: 87.4 us -> none  [local(): gram, cross_sum = lax.psum((gram_part, cross_part), ('gx', 'gy'))]
    pallas_call x0 -> x4, Pallas kernels: none -> 68.4 us  [the longest x1 22.2 us: run_model(): pl.pallas_call(functools.partial(model_kernel, mesh.shape['gy'], rows), g...]
    mul x18 -> x0, other arithmetic: 23.2 us -> none  [the longest x4 13.6 us: local(): extended = field_wide * wall_mask(rows_here, margin)]
    another operation x5 -> x0, other arithmetic: 22.9 us -> none  [the longest x3 12.4 us: local(): factor = jnp.linalg.cholesky(system)]
    ppermute x4 -> x0, waiting for transfers between devices: 21.4 us -> none  [the longest x2 19.2 us: with_halo(): lax.ppermute(lax.slice_in_dim(block, block.shape[dim] - width, None, axis...]
    all_gather x2 -> x0, blocking collectives: 9.36 us -> none  [the longest x1 5 us: local(): lax.all_gather(observed_here, 'ens', axis=0, tiled=True)]
    ppermute x4 -> x0, starting transfers between devices: 6.9 us -> none  [the longest x2 3.8 us: with_halo(): lax.ppermute(lax.slice_in_dim(block, 0, width, axis=dim), axis, backward)]
    slice x10 -> x0, local copies, waits for them, and re-layouts: 6.79 us -> none  [the longest x4 4.63 us: with_halo(): lax.slice_in_dim(block, block.shape[dim] - width, None, axis=dim)]
  transfers between devices with their start and end apart: 5 -> 0, of which waited for: 5 -> 0; matrix products, arithmetic and copies ran while one was open for 2% -> 0% of each run, Pallas kernels for 0% -> 0%
where the time goes in v1:
time: 75.3 us; the launch traced here: 74.8 us
  Pallas kernels  68.4 us (91%)
  local copies, waits for them, and re-layouts  5.68 us (8%)
    pallas_call x1, Pallas kernels, run_model(): pl.pallas_call(functools.partial(model_kernel, mesh.shape['gy'], rows), g...  22.2 us
    pallas_call x1, Pallas kernels, ensemble_sums(): pl.pallas_call(functools.partial(sums_kernel, n_gx, n_gy, n_ens, reduce_h...  22 us
    pallas_call x1, Pallas kernels, halo_exchange(): pl.pallas_call(functools.partial(halo_kernel, mesh.shape['gx'], mesh.shap...  12.2 us
    pallas_call x1, Pallas kernels, solve(): pl.pallas_call(functools.partial(solve_kernel, theta.shape[0]), out_shape...  12.1 us
    unnamed x13, local copies, waits for them, and re-layouts  5.67 us

profile of v1, /device:TPU:0, one launch (start us, length us, event | category | flops | bytes accessed | tf_op | source)
XLA Modules:
  0.0 74.8 jit_solution(10665119455323190302)
XLA Ops:
  0.6 1.4 %copy.12.theta_ref = f32[64,4]{1,0:T(8,128)} copy(f32[64,4]{0,1:T(4,128)} %param.16) | data formatting | bytes 2048 | tf_op args[6]
  2.0 0.0 copy-start.1
  2.0 0.9 %constant_dynamic-update-slice_fusion.3 = f32[16,16,128]{2,1,0:T(8,128)S(1)} fusion(f32[8,16,128]{2,1,0:T(8,128)} %param.14), kind=kLoop, calls=%fused_computation.4 | loop fusion | bytes 131072
  2.9 0.0 copy-done.1
  2.9 0.0 copy-start.2
  2.9 0.7 copy-done.2
  3.6 0.0 copy-start.3
  3.6 0.7 copy-done.3
  4.3 0.0 copy-start
  4.3 0.6 copy-done
  4.9 12.2 %halo.1 = (f32[64,8,128]{2,1,0:T(8,128)}, f32[64,8,128]{2,1,0:T(8,128)}, f32[16,8,128]{2,1,0:T(8,128)}, f32[16,8,128]{2,1,0:T(8,128)}, f32[2,80,128]{2,1,0:T(8,1...) custom-call(f32[64,16,128]{2,1,0:T(8,128)} %q_ref.1, f32[16,16,128]{2,1,0:T(8,128)} %copy-done), custom_call_target="tpu_custom_call" | custom-call | tf_op jit(solution)/shard_map/halo/pallas_call | solution.py:118
  17.1 22.2 %model.1 = (f32[1024,128]{1,0:T(8,128)}, f32[64,128]{1,0:T(8,128)}, f32[64,128]{1,0:T(8,128)}) custom-call(f32[1024,128]{1,0:T(8,128)} %bitcast.13, f32[512,128]{1,0:T(8,128)} %bitcast.15, f32[512,128]{1,0:T(8,128)} %bitcast.16, f32[2,80,128]{2,1,0:T(8,128)} %get-tuple-element.16.mid_ref.fmid_ref, f32[2,80,128]{2,1,0:T(8,128)} %get-tuple-element.17.top_ref.ftop_ref, ...), custom_call_target="tpu_custom_call" | custom-call | tf_op jit(solution)/shard_map/model/pallas_call | solution.py:275
  39.3 22.0 %sums.1 = (f32[128,256]{1,0:T(8,128)}, f32[128,128]{1,0:T(8,128)}) custom-call(f32[64,128]{1,0:T(8,128)} %get-tuple-element.22.obs_ref, f32[64,128]{1,0:T(8,128)} %get-tuple-element.23.thp_ref, f32[1,1,128]{2,1,0:T(1,128)} %val_ref.1, f32[1,1,128]{2,1,0:T(1,128)} %sig_ref.1), custom_call_target="tpu_custom_call" | custom-call | tf_op jit(solution)/shard_map/sums/pallas_call | solution.py:370
  61.3 12.1 %solve.1 = f32[64,4]{1,0:T(8,128)} custom-call(f32[128,256]{1,0:T(8,128)} %get-tuple-element.24.full_ref, f32[128,128]{1,0:T(8,128)} %get-tuple-element.25.th_ref), custom_call_target="tpu_custom_call" | custom-call | tf_op jit(solution)/shard_map/solve/pallas_call | solution.py:427
  73.4 1.4 %copy.13 = f32[64,4]{0,1:T(4,128)} copy(f32[64,4]{1,0:T(8,128)} %solve.1) | data formatting | bytes 2048
  (4 shorter events, 0.0 us)
Async XLA Ops:
  2.0 0.9 %copy-start.1 = (f32[16,128]{1,0:T(8,128)S(1)}, f32[16,128]{1,0:T(8,128)}, u32[]{:S(2)}) copy-start(f32[16,128]{1,0:T(8,128)} %param.11) | copy-start | bytes 24580
  2.9 0.7 copy-start.2
  3.6 0.7 copy-start.3
  4.3 0.6 copy-start

commit v2 on v1

--- a/solution.py
+++ b/solution.py
@@ -130,165 +130,257 @@
     )(state, fields)
 
 
-def model_kernel(n_gy, rows, q_ref, qt_ref, qb_ref, mid_ref, top_ref, bot_ref,
-                 f_ref, ft_ref, fb_ref, fmid_ref, ftop_ref, fbot_ref,
+def model_kernel(n_gy, q_ref, qt_ref, qb_ref, f_ref, ft_ref, fb_ref, mid_ref, top_ref, bot_ref,
                  mode_ref, theta_ref, index_ref, out_ref, obs_ref, thp_ref,
-                 Q, FO, FP, ST):
-    g = pl.program_id(0)
+                 Q, L, FO, US, H, LH, FH, UH, TH):
     gy = lax.axis_index("gy")
-    cols = 128
+    members = mode_ref.shape[1]
+    cols = q_ref.shape[1]
+    rows = q_ref.shape[0] // members
+    n_rows = rows + 2 * DEPTH
     has_up, has_down = gy > 0, gy < n_gy - 1
-    n_rows = rows + 2 * DEPTH
     shape = (8, cols)
     lane = lax.broadcasted_iota(jnp.int32, shape, 1)
     sub = lax.broadcasted_iota(jnp.int32, shape, 0)
+    half_ok = jnp.where(lane < cols // 2, has_down.astype(jnp.int32), has_up.astype(jnp.int32)) > 0
+    bits = {k: jnp.bitwise_and(lane, k) != 0 for k in (1, 2, 4)}
+
+    def roll(x, k):
+        return pltpu.roll(x, k % cols, 1)
+
+    def butterfly(xs):
+        xs = list(xs)
+        for k in (1, 2, 4):
+            for v in range(8):
+                if not v & k:
+                    x, y = xs[v], xs[v | k]
+                    xs[v] = jnp.where(bits[k], roll(y, k), x)
+                    xs[v | k] = jnp.where(bits[k], y, roll(x, -k))
+        return xs
+
+    def masked(i, x):
+        if i < DEPTH:
+            return jnp.where(has_up, x, 0.0)
+        if i >= DEPTH + rows:
+            return jnp.where(has_down, x, 0.0)
+        return x
+
+    def masked_half(half, x):
+        return jnp.where(half_ok, x, 0.0) if half else x
+
+    def gather(x, idx, axis):
+        return jnp.take_along_axis(x, idx, axis=axis, mode="promise_in_bounds")
+
+    def strip(side, half, pick):
+        if half:
+            x = jnp.where(lane < cols // 2, pick(bot_ref, side), pick(top_ref, side))
+            return masked_half(1, x)
+        return pick(mid_ref, side)
+
+    TH[...] = jnp.zeros_like(TH)
+    TH[0:theta_ref.shape[0], 0:members] = theta_ref[...]
+    thp_ref[...] = TH[...].T[0:members]
+    slot = sub * 8 + jnp.bitwise_and(lane, 7)
+    par = [gather(jnp.broadcast_to(TH[k:k + 1, :], shape), slot, 1) for k in range(4)]
+    diffuse = 0.05 * (1.0 + 0.5 * jnp.tanh(par[0]))
+    hyper = 0.005 * (1.0 + 0.5 * jnp.tanh(par[1]))
+    keep = 1.0 - 0.05 * (1.0 + 0.5 * jnp.tanh(par[2]))
+    gain = par[3]
+    mrow = jnp.concatenate([mode_ref[...], jnp.zeros((1, cols - members), jnp.int32)], axis=1)
+    mrow = jnp.broadcast_to(mrow, shape)
+    modes = [gather(mrow, sub * 8 + v, 1) for v in range(8)]
+
+    block0 = lane - jnp.bitwise_and(lane, 7)
+    for f in range(3):
+        for j in range(n_rows // 8):
+            if j == 0:
+                x = jnp.where(has_up, ft_ref[pl.ds((8 + f) * DEPTH, 8), :], 0.0)
+            elif j == n_rows // 8 - 1:
+                x = jnp.where(has_down, fb_ref[pl.ds((8 + f) * DEPTH, 8), :], 0.0)
+            else:
+                x = f_ref[pl.ds((8 + f) * rows + (j - 1) * 8, 8), :]
+            x = x if f == 2 else 0.5 * x
+            for c in range(8):
+                US[f, c, pl.ds(j * 8, 8), :] = gather(x, block0 + c, 1)
+    scale = jnp.where(sub < 2, 0.5, 1.0)
+    for side in range(2):
+        for half in range(2):
+            x = scale * strip(side, half, lambda ref, sd: ref[sd, members + 8:members + 16, :])
+            for c in range(8):
+                UH[side, c, half] = gather(x, block0 + c, 1)
+            x = strip(side, half, lambda ref, sd: ref[sd, members:members + 8, :])
+            ys = butterfly([gather(x, modes[v], 0) for v in range(8)])
+            for c in range(8):
+                FH[side, c, half] = gain * ys[c]
+            ys = butterfly([strip(side, half, lambda ref, sd: ref[sd, pl.ds(v, 8, stride=8), :]) for v in range(8)])
+            for c in range(8):
+                H[0, side, c, half] = ys[c]
+
+    for i in range(n_rows):
+        if i < DEPTH:
+            ref, per, k, fr = qt_ref, DEPTH, i, ft_ref
+        elif i < DEPTH + rows:
+            ref, per, k, fr = q_ref, rows, i - DEPTH, f_ref
+        else:
+            ref, per, k, fr = qb_ref, DEPTH, i - DEPTH - rows, fb_ref
+        ys = butterfly([masked(i, ref[pl.ds(v * per + k, 8, stride=8 * per), :]) for v in range(8)])
+        for c in range(8):
+            Q[0, i, c] = ys[c]
+        if 2 <= i < n_rows - 2:
+            x = masked(i, fr[pl.ds(k, 8, stride=per), :])
+            ys = butterfly([gather(x, modes[v], 0) for v in range(8)])
+            for c in range(8):
+                FO[i, c] = gain * ys[c]
+
+    first, last = lane < 8, lane >= cols - 8
+
+    def place(i):
+        j = i - DEPTH
+        return (0, j) if 0 <= j < rows else (1, (i - DEPTH - rows) % n_rows)
+
+    def across(x, get, i):
+        half, j = place(i)
+        left = jnp.where(first, roll(get(0, 7, half), -8 * j), roll(x(7), 8))
+        right = jnp.where(last, roll(get(1, 0, half), cols - 8 - 8 * j), roll(x(0), -8))
+        return left, right
+
+    def inward(x, lo, hi):
+        left = [jnp.zeros(shape, F32)] * 2
+        right = [jnp.zeros(shape, F32)] * 2
+        for i in range(lo, hi):
+            half, j = place(i)
+            here = block0 == 8 * j
+            left[half] = jnp.where(here, roll(x(i, 0), 8 * j), left[half])
+            right[half] = jnp.where(here, roll(x(i, 7), 8 * j - (cols - 8)), right[half])
+        return left, right
+
+    def vertical(m, t):
+        mn, tn, mp, tp = roll(m, -8), roll(t, -8), roll(m, 8), roll(t, 8)
+        return ((jnp.where(last, tn, mn), jnp.where(last, mn, tn)),
+                (jnp.where(first, tp, mp), jnp.where(first, mp, tp)))
+
     zero = jnp.zeros(shape, F32)
 
-    def inside(i):
-        return has_up if i < DEPTH else (has_down if i >= DEPTH + rows else None)
-
-    def masked(i, x):
-        ok = inside(i)
-        return x if ok is None else jnp.where(ok, x, 0.0)
-
-    def row_pair(i, base, q, qt, qb, mid, top, bot, mbase):
-        if i < DEPTH:
-            a = qt[pl.ds(base * DEPTH + i, 8, stride=DEPTH), :]
-            strip, k = top, rows - DEPTH + i
-        elif i < DEPTH + rows:
-            a = q[pl.ds(base * rows + i - DEPTH, 8, stride=rows), :]
-            strip, k = mid, i - DEPTH
+    def halo_x(get, ins, side, c, half):
+        left, right = ins
+        if c > 0:
+            xm = get(side, c - 1, half)
         else:
-            a = qb[pl.ds(base * DEPTH + i - DEPTH - rows, 8, stride=DEPTH), :]
-            strip, k = bot, i - DEPTH - rows
-        lo = pltpu.roll(strip[0, mbase:mbase + 8, :], (cols - DEPTH - k * DEPTH) % cols, 1)
-        hi = pltpu.roll(strip[1, mbase:mbase + 8, :], (cols - k * DEPTH) % cols, 1)
-        b = jnp.where(lane < DEPTH, hi, jnp.where(lane >= cols - DEPTH, lo, 0.0))
-        return masked(i, a), masked(i, b)
-
-    @pl.when(g == 0)
-    def _():
-        for i in range(n_rows):
-            pa, pb = row_pair(i, 0, f_ref, ft_ref, fb_ref, fmid_ref, ftop_ref, fbot_ref, 0)
-            FP[i, 0] = pa
-            FP[i, 1] = pb
-            sa, sb = row_pair(i, 8, f_ref, ft_ref, fb_ref, fmid_ref, ftop_ref, fbot_ref, 8)
-            for h, s in ((0, sa), (1, sb)):
-                ST[0, i, h] = jnp.broadcast_to(0.5 * s[0:1], shape)
-                ST[1, i, h] = jnp.broadcast_to(0.5 * s[1:2], shape)
-                ST[2, i, h] = jnp.broadcast_to(s[2:3], shape)
-
-    th = theta_ref[...]
-    diffuse = jnp.broadcast_to(0.05 * (1.0 + 0.5 * jnp.tanh(th[:, 0:1])), shape)
-    hyper = jnp.broadcast_to(0.005 * (1.0 + 0.5 * jnp.tanh(th[:, 1:2])), shape)
-    keep = jnp.broadcast_to(1.0 - 0.05 * (1.0 + 0.5 * jnp.tanh(th[:, 2:3])), shape)
-    gain = jnp.broadcast_to(th[:, 3:4], shape)
-    thp = zero
-    for k in range(th.shape[1]):
-        thp = jnp.where(lane == k, th[:, k:k + 1], thp)
-    thp_ref[...] = thp
-
-    mode = jnp.zeros(shape, jnp.int32)
-    for k in range(8):
-        mode = jnp.where(sub == k, mode_ref[g * 8 + k], mode)
-
-    for i in range(n_rows):
-        a, b = row_pair(i, 0, q_ref, qt_ref, qb_ref, mid_ref, top_ref, bot_ref, 0)
-        Q[0, i, 0] = a
-        Q[0, i, 1] = b
-        if 2 <= i < n_rows - 2:
-            for h in range(2):
-                FO[i, h] = gain * jnp.take_along_axis(FP[i, h], mode, axis=0, mode="promise_in_bounds")
-
-    first, last = lane == 0, lane == cols - 1
-
-    def neighbours(a, b):
-        ap, bp = pltpu.roll(a, cols - 1, 1), pltpu.roll(b, cols - 1, 1)
-        am, bm = pltpu.roll(a, 1, 1), pltpu.roll(b, 1, 1)
-        return ((jnp.where(last, bp, ap), jnp.where(first, bm, am)),
-                (jnp.where(last, ap, bp), jnp.where(first, am, bm)))
+            xm = right[half] if side == 1 else zero
+        if c < 7:
+            xp = get(side, c + 1, half)
+        else:
+            xp = left[half] if side == 0 else zero
+        return xm, xp
 
     for s in range(STEPS):
         src, dst = s % 2, (s + 1) % 2
         lo, hi = 2 * s, n_rows - 2 * s
         final = s == STEPS - 1
-        q, lap, grad = {}, {}, {}
-
-        def load(i):
-            q[i] = (Q[src, i, 0], Q[src, i, 1])
-
-        def make_lap(i):
-            pair = neighbours(*q[i])
-            both, gr = [], []
-            for h in range(2):
-                xp, xm = pair[h]
-                v = (q[i + 1][h] + q[i - 1][h]) + (xp + xm) - 4.0 * q[i][h]
-                both.append(masked(i, v))
-                gr.append(xp - xm)
-            lap[i], grad[i] = tuple(both), gr
-
-        load(lo)
-        load(lo + 1)
-        for i in range(lo + 2, lo + 4):
-            load(i)
-            make_lap(i - 1)
+        qa = lambda i, c: Q[src, i, c]
+        qh = lambda side, c, half: H[src, side, c, half]
+        lh = lambda side, c, half: LH[side, c, half]
+        la = lambda i, c: L[i, c]
+        ins = inward(qa, lo, hi)
+        grads = {}
+        for side in range(2):
+            for c in range(8):
+                m, t = qh(side, c, 0), qh(side, c, 1)
+                nxt, prv = vertical(m, t)
+                for half in range(2):
+                    mid = (m, t)[half]
+                    xm, xp = halo_x(qh, ins, side, c, half)
+                    lap = (nxt[half] + prv[half]) + (xp + xm) - 4.0 * mid
+                    LH[side, c, half] = masked_half(half, lap)
+                    if not final:
+                        grads[side, c, half] = (UH[side, c, half, 0:1] * (xp - xm)
+                                                + UH[side, c, half, 1:2] * (nxt[half] - prv[half]))
+        adv = {}
+        def first_pass(i):
+            left, right = across(lambda c: qa(i, c), qh, i)
+            row = [qa(i, c) for c in range(8)]
+            for c in range(8):
+                xm = row[c - 1] if c else left
+                xp = row[c + 1] if c < 7 else right
+                up, dn = qa(i + 1, c), qa(i - 1, c)
+                L[i, c] = masked(i, (up + dn) + (xp + xm) - 4.0 * row[c])
+                if lo + 2 <= i < hi - 2:
+                    adv[i, c] = (US[0, c, i:i + 1, :] * (xp - xm) + US[1, c, i:i + 1, :] * (up - dn))
+                    adv[i, c] = keep * row[c] + (FO[i, c] - adv[i, c])
+
+        def second_pass(i):
+            left, right = across(lambda c: la(i, c), lh, i)
+            row = [la(i, c) for c in range(8)]
+            outs = []
+            for c in range(8):
+                xm = row[c - 1] if c else left
+                xp = row[c + 1] if c < 7 else right
+                bi = (la(i + 1, c) + la(i - 1, c)) + (xp + xm) - 4.0 * row[c]
+                new = (adv.pop((i, c)) + (diffuse * row[c] - hyper * bi)) * US[2, c, i:i + 1, :]
+                if final:
+                    outs.append(new)
+                else:
+                    Q[dst, i, c] = new
+            if final:
+                for v, y in enumerate(butterfly(outs)):
+                    out_ref[pl.ds(v * rows + i - DEPTH, 8, stride=8 * rows), :] = y
+
+        first_pass(lo + 1)
+        first_pass(lo + 2)
         for i in range(lo + 2, hi - 2):
-            load(i + 2) if i + 2 < hi else None
-            make_lap(i + 1)
-            pair = neighbours(*lap[i])
-            for h in range(1 if final else 2):
-                xp, xm = pair[h]
-                bi = (lap[i + 1][h] + lap[i - 1][h]) + (xp + xm) - 4.0 * lap[i][h]
-                adv = ST[0, i, h] * grad[i][h] + ST[1, i, h] * (q[i + 1][h] - q[i - 1][h])
-                new = keep * q[i][h] + diffuse * lap[i][h] - hyper * bi + (FO[i, h] - adv)
-                new = new * ST[2, i, h]
-                if final:
-                    out_ref[pl.ds(i - DEPTH, 8, stride=rows), :] = new
-                else:
-                    Q[dst, i, h] = new
+            first_pass(i + 1)
+            second_pass(i)
+        if final:
+            break
+        ins = inward(la, lo + 1, hi - 1)
+        for side in range(2):
+            for c in range(8):
+                m, t = lh(side, c, 0), lh(side, c, 1)
+                nxt, prv = vertical(m, t)
+                for half in range(2):
+                    mid = (m, t)[half]
+                    xm, xp = halo_x(lh, ins, side, c, half)
+                    bi = (nxt[half] + prv[half]) + (xp + xm) - 4.0 * mid
+                    new = (keep * qh(side, c, half) + (FH[side, c, half] - grads[side, c, half])
+                           + (diffuse * mid - hyper * bi))
+                    H[dst, side, c, half] = new * UH[side, c, half, 2:3]
 
     index = index_ref[0]
     col = jnp.bitwise_and(index, cols - 1)
     row = jnp.right_shift(index, cols.bit_length() - 1)
     hot = (lax.broadcasted_iota(jnp.int32, (cols, cols), 0) == col).astype(jnp.bfloat16)
-    x = out_ref[...]
-    x1 = x.astype(jnp.bfloat16)
-    rem = x - x1.astype(F32)
-    x2 = rem.astype(jnp.bfloat16)
-    x3 = (rem - x2.astype(F32)).astype(jnp.bfloat16)
+    row_id = lax.broadcasted_iota(jnp.int32, (8, rows, cols), 1)
     dot = functools.partial(jnp.dot, preferred_element_type=F32)
-    picked = dot(x1, hot) + (dot(x2, hot) + dot(x3, hot))
-    row_id = lax.broadcasted_iota(jnp.int32, (8, rows, cols), 1)
-    obs_ref[...] = jnp.sum(jnp.where(row_id == row[None], picked.reshape(8, rows, cols), 0.0), axis=1)
+    for g in range(members // 8):
+        x = out_ref[pl.ds(g * 8 * rows, 8 * rows), :]
+        x1 = x.astype(jnp.bfloat16)
+        rem = x - x1.astype(F32)
+        x2 = rem.astype(jnp.bfloat16)
+        x3 = (rem - x2.astype(F32)).astype(jnp.bfloat16)
+        picked = dot(x1, hot) + (dot(x2, hot) + dot(x3, hot))
+        obs_ref[pl.ds(g * 8, 8), :] = jnp.sum(
+            jnp.where(row_id == row[None], picked.reshape(8, rows, cols), 0.0), axis=1)
 
 
 def run_model(mesh, state, fields, halos, member_mode, theta, obs_index):
     members, rows, cols = state.shape
-    nf = fields.shape[0]
     qt, qb, ft, fb, mid, top, bot = halos
     n_rows = rows + 2 * DEPTH
     sds = jax.ShapeDtypeStruct
-    by_group = lambda n: pl.BlockSpec((8 * n, cols), lambda g: (g, 0))
-    strip = pl.BlockSpec((2, 8, cols), lambda g: (0, g, 0))
-    fstrip = pl.BlockSpec((2, nf, cols), lambda g: (0, members // nf, 0))
-    whole = lambda n: pl.BlockSpec((nf * n, cols), lambda g: (0, 0))
+    reg = (8, cols)
     out, obs, thp = pl.pallas_call(
-        functools.partial(model_kernel, mesh.shape["gy"], rows),
-        grid=(members // 8,),
+        functools.partial(model_kernel, mesh.shape["gy"]),
         out_shape=[sds((members * rows, cols), F32), sds((members, cols), F32), sds((members, cols), F32)],
-        in_specs=[by_group(rows), by_group(DEPTH), by_group(DEPTH), strip, strip, strip,
-                  whole(rows), whole(DEPTH), whole(DEPTH), fstrip, fstrip, fstrip,
-                  pl.BlockSpec(memory_space=pltpu.SMEM),
-                  pl.BlockSpec((8, theta.shape[1]), lambda g: (g, 0)),
-                  pl.BlockSpec((1, 1, obs_index.shape[-1]), lambda g: (0, 0, 0))],
-        out_specs=[by_group(rows), pl.BlockSpec((8, cols), lambda g: (g, 0)),
-                   pl.BlockSpec((8, cols), lambda g: (g, 0))],
-        scratch_shapes=[VM((2, n_rows, 2, 8, cols), F32), VM((n_rows, 2, 8, cols), F32),
-                        VM((n_rows, 2, 8, cols), F32), VM((3, n_rows, 2, 8, cols), F32)],
+        in_specs=[vspec()] * 12,
+        out_specs=[vspec()] * 3,
+        scratch_shapes=[VM((2, n_rows, 8) + reg, F32), VM((n_rows, 8) + reg, F32), VM((n_rows, 8) + reg, F32),
+                        VM((3, 8, n_rows, cols), F32),
+                        VM((2, 2, 8, 2) + reg, F32), VM((2, 8, 2) + reg, F32), VM((2, 8, 2) + reg, F32),
+                        VM((2, 8, 2) + reg, F32), VM((cols, cols), F32)],
         name="model",
-    )(state.reshape(members * rows, cols), qt.reshape(-1, cols), qb.reshape(-1, cols), mid, top, bot,
+    )(state.reshape(members * rows, cols), qt.reshape(-1, cols), qb.reshape(-1, cols),
       fields.reshape(-1, cols), ft.reshape(-1, cols), fb.reshape(-1, cols), mid, top, bot,
-      member_mode, theta, obs_index)
+      member_mode.reshape(1, members), theta.T, obs_index)
     return out.reshape(members, rows, cols), obs, thp
 
 
@@ -420,18 +512,19 @@
     ens = lax.axis_index("ens")
     x = xs[pl.ds(pl.multiple_of(ens * members, members), members), :]
     new = mean + shift + float(total - 1) * x
-    out_ref[...] = new[:, 0:out_ref.shape[1]]
+    xs[0:members, :] = new
+    out_ref[...] = xs[...].T[0:out_ref.shape[0], 0:members]
 
 
 def solve(full, th, theta):
     return pl.pallas_call(
         functools.partial(solve_kernel, theta.shape[0]),
-        out_shape=jax.ShapeDtypeStruct(theta.shape, F32),
+        out_shape=jax.ShapeDtypeStruct(theta.shape[::-1], F32),
         in_specs=[vspec()] * 2,
         out_specs=vspec(),
         scratch_shapes=[VM(th.shape, F32)],
         name="solve",
-    )(full, th)
+    )(full, th).T
 
 
 def local(mesh, state, u_vel, v_vel, land, forcing, member_mode, theta, obs_index, obs_values, obs_sigma):

time: 75.3 us -> 67.9 us (0.902)
  Pallas kernels: 68.4 us -> 63.9 us
  local copies, waits for them, and re-layouts: 5.68 us -> 2.88 us
    pallas_call x1, Pallas kernels: 22.2 us -> 17.8 us  [run_model(): pl.pallas_call(functools.partial(model_kernel, mesh.shape['gy']), out_sha...]
    unnamed x13 -> x11, local copies, waits for them, and re-layouts: 5.67 us -> 2.88 us
where the time goes in v2:
time: 67.9 us; the launch traced here: 67.5 us
  Pallas kernels  63.9 us (94%)
  local copies, waits for them, and re-layouts  2.88 us (4%)
    pallas_call x1, Pallas kernels, ensemble_sums(): pl.pallas_call(functools.partial(sums_kernel, n_gx, n_gy, n_ens, reduce_h...  22 us
    pallas_call x1, Pallas kernels, run_model(): pl.pallas_call(functools.partial(model_kernel, mesh.shape['gy']), out_sha...  17.8 us
    pallas_call x1, Pallas kernels, halo_exchange(): pl.pallas_call(functools.partial(halo_kernel, mesh.shape['gx'], mesh.shap...  12.2 us
    pallas_call x1, Pallas kernels, solve(): pl.pallas_call(functools.partial(solve_kernel, theta.shape[0]), out_shape...  12.1 us
    unnamed x11, local copies, waits for them, and re-layouts  2.88 us

profile of v2, /device:TPU:0, one launch (start us, length us, event | category | flops | bytes accessed | tf_op | source)
XLA Modules:
  0.0 67.5 jit_solution(15458049402802647031)
XLA Ops:
  0.6 0.0 copy-start.1
  0.6 0.9 %constant_dynamic-update-slice_fusion.3 = f32[16,16,128]{2,1,0:T(8,128)S(1)} fusion(f32[8,16,128]{2,1,0:T(8,128)} %param.14), kind=kLoop, calls=%fused_computation.4 | loop fusion | bytes 131072
  1.5 0.0 copy-done.1
  1.5 0.0 copy-start.2
  1.5 0.7 %copy-done.2 = f32[16,128]{1,0:T(8,128)S(1)} copy-done((f32[16,128]{1,0:T(8,128)S(1)}, f32[16,128]{1,0:T(8,128)}, u32[]{:S(2)}) %copy-start.2) | copy-done | bytes 8216
  2.2 0.0 copy-start.3
  2.2 0.7 %copy-done.3 = s32[16,128]{1,0:T(8,128)S(1)} copy-done((s32[16,128]{1,0:T(8,128)S(1)}, s32[16,128]{1,0:T(8,128)}, u32[]{:S(2)}) %copy-start.3) | copy-done | bytes 8216
  2.9 0.0 copy-start
  2.9 0.6 copy-done
  3.5 12.2 %halo.1 = (f32[64,8,128]{2,1,0:T(8,128)}, f32[64,8,128]{2,1,0:T(8,128)}, f32[16,8,128]{2,1,0:T(8,128)}, f32[16,8,128]{2,1,0:T(8,128)}, f32[2,80,128]{2,1,0:T(8,1...) custom-call(f32[64,16,128]{2,1,0:T(8,128)} %q_ref.1, f32[16,16,128]{2,1,0:T(8,128)} %copy-done), custom_call_target="tpu_custom_call" | custom-call | tf_op jit(solution)/shard_map/halo/pallas_call | solution.py:118
  15.7 17.8 %model.1 = (f32[1024,128]{1,0:T(8,128)}, f32[64,128]{1,0:T(8,128)}, f32[64,128]{1,0:T(8,128)}) custom-call(f32[1024,128]{1,0:T(8,128)} %bitcast.16, f32[512,128]{1,0:T(8,128)} %bitcast.18, f32[512,128]{1,0:T(8,128)} %bitcast.19, f32[256,128]{1,0:T(8,128)} %bitcast.17, f32[128,128]{1,0:T(8,128)} %bitcast.20, f32[128,128]{1,0:T(8,128)} %bitcast.21, ...), custom_call_target="tpu_custom_call" | custom-call | tf_op jit(solution)/shard_map/model/pallas_call | solution.py:371
  33.5 22.0 %sums.1 = (f32[128,256]{1,0:T(8,128)}, f32[128,128]{1,0:T(8,128)}) custom-call(f32[64,128]{1,0:T(8,128)} %get-tuple-element.22.obs_ref, f32[64,128]{1,0:T(8,128)} %get-tuple-element.23.thp_ref, f32[1,1,128]{2,1,0:T(1,128)} %val_ref.1, f32[1,1,128]{2,1,0:T(1,128)} %sig_ref.1), custom_call_target="tpu_custom_call" | custom-call | tf_op jit(solution)/shard_map/sums/pallas_call | solution.py:462
  55.5 12.1 %solve.1 = f32[4,64]{1,0:T(4,128)} custom-call(f32[128,256]{1,0:T(8,128)} %get-tuple-element.24.full_ref, f32[128,128]{1,0:T(8,128)} %get-tuple-element.25.th_ref), custom_call_target="tpu_custom_call" | custom-call | tf_op jit(solution)/shard_map/solve/pallas_call | solution.py:520
  (4 shorter events, 0.0 us)
Async XLA Ops:
  0.6 0.9 %copy-start.1 = (f32[16,128]{1,0:T(8,128)S(1)}, f32[16,128]{1,0:T(8,128)}, u32[]{:S(2)}) copy-start(f32[16,128]{1,0:T(8,128)} %param.11) | copy-start | bytes 24580
  1.5 0.7 %copy-start.2 = (f32[16,128]{1,0:T(8,128)S(1)}, f32[16,128]{1,0:T(8,128)}, u32[]{:S(2)}) copy-start(f32[16,128]{1,0:T(8,128)} %param.12) | copy-start | bytes 24580
  2.2 0.7 %copy-start.3 = (s32[16,128]{1,0:T(8,128)S(1)}, s32[16,128]{1,0:T(8,128)}, u32[]{:S(2)}) copy-start(s32[16,128]{1,0:T(8,128)} %param.13) | copy-start | bytes 24580
  2.9 0.6 copy-start

commit v3 on v2

--- a/solution.py
+++ b/solution.py
@@ -18,7 +18,7 @@
     return pl.BlockSpec(memory_space=pltpu.VMEM)
 
 
-def halo_kernel(n_gx, n_gy, q_ref, f_ref, qt_ref, qb_ref, ft_ref, fb_ref, mid_ref, top_ref, bot_ref,
+def halo_kernel(n_gx, n_gy, q_ref, forcing_ref, u_ref, v_ref, land_ref, f_ref, qt_ref, qb_ref, ft_ref, fb_ref, mid_ref, top_ref, bot_ref,
                 pack, row_send, row_recv, gx_send, gx_recv, gy_send, gy_recv):
     gx, gy = lax.axis_index("gx"), lax.axis_index("gy")
     right, left = lax.rem(gx + 1, n_gx), lax.rem(gx + n_gx - 1, n_gx)
@@ -26,6 +26,13 @@
     up, down = jnp.maximum(gy - 1, 0), jnp.minimum(gy + 1, n_gy - 1)
     members, rows, cols = q_ref.shape
     fields = f_ref.shape[0]
+
+    patterns = forcing_ref.shape[0]
+    f_ref[0:patterns] = forcing_ref[...]
+    f_ref[patterns] = u_ref[...]
+    f_ref[patterns + 1] = v_ref[...]
+    f_ref[patterns + 2] = (1 - land_ref[...]).astype(F32)
+    f_ref[patterns + 3:] = jnp.zeros((fields - patterns - 3, rows, cols), F32)
 
     barrier = pltpu.get_barrier_semaphore()
     pl.semaphore_signal(barrier, inc=1, device_id={"gx": right}, device_id_type=MESH)
@@ -110,28 +117,28 @@
             c.wait_recv()
 
 
-def halo_exchange(mesh, state, fields):
+def halo_exchange(mesh, state, forcing, u_vel, v_vel, land):
     members, rows, cols = state.shape
-    nf = fields.shape[0]
+    nf = 16
     total = members + nf
     sds = jax.ShapeDtypeStruct
     return pl.pallas_call(
         functools.partial(halo_kernel, mesh.shape["gx"], mesh.shape["gy"]),
-        out_shape=[sds((members, DEPTH, cols), F32), sds((members, DEPTH, cols), F32),
+        out_shape=[sds((nf, rows, cols), F32), sds((members, DEPTH, cols), F32), sds((members, DEPTH, cols), F32),
                    sds((nf, DEPTH, cols), F32), sds((nf, DEPTH, cols), F32),
                    sds((2, total, cols), F32), sds((2, total, cols), F32), sds((2, total, cols), F32)],
-        in_specs=[vspec()] * 2,
-        out_specs=[vspec()] * 7,
+        in_specs=[vspec()] * 5,
+        out_specs=[vspec()] * 8,
         scratch_shapes=[VM((2, total, cols), F32)]
         + [pltpu.SemaphoreType.DMA((4,))] * 2
         + [pltpu.SemaphoreType.DMA((2,))] * 4,
         compiler_params=pltpu.CompilerParams(collective_id=0, has_side_effects=True),
         name="halo",
-    )(state, fields)
+    )(state, forcing, u_vel, v_vel, land)
 
 
 def model_kernel(n_gy, q_ref, qt_ref, qb_ref, f_ref, ft_ref, fb_ref, mid_ref, top_ref, bot_ref,
-                 mode_ref, theta_ref, index_ref, out_ref, obs_ref, thp_ref,
+                 mode_ref, theta_ref, index_ref, out_ref, obs_ref,
                  Q, L, FO, US, H, LH, FH, UH, TH):
     gy = lax.axis_index("gy")
     members = mode_ref.shape[1]
@@ -179,7 +186,6 @@
 
     TH[...] = jnp.zeros_like(TH)
     TH[0:theta_ref.shape[0], 0:members] = theta_ref[...]
-    thp_ref[...] = TH[...].T[0:members]
     slot = sub * 8 + jnp.bitwise_and(lane, 7)
     par = [gather(jnp.broadcast_to(TH[k:k + 1, :], shape), slot, 1) for k in range(4)]
     diffuse = 0.05 * (1.0 + 0.5 * jnp.tanh(par[0]))
@@ -368,24 +374,24 @@
     n_rows = rows + 2 * DEPTH
     sds = jax.ShapeDtypeStruct
     reg = (8, cols)
-    out, obs, thp = pl.pallas_call(
+    out, obs = pl.pallas_call(
         functools.partial(model_kernel, mesh.shape["gy"]),
-        out_shape=[sds((members * rows, cols), F32), sds((members, cols), F32), sds((members, cols), F32)],
+        out_shape=[sds((members * rows, cols), F32), sds((members, cols), F32)],
         in_specs=[vspec()] * 12,
-        out_specs=[vspec()] * 3,
+        out_specs=[vspec()] * 2,
         scratch_shapes=[VM((2, n_rows, 8) + reg, F32), VM((n_rows, 8) + reg, F32), VM((n_rows, 8) + reg, F32),
                         VM((3, 8, n_rows, cols), F32),
                         VM((2, 2, 8, 2) + reg, F32), VM((2, 8, 2) + reg, F32), VM((2, 8, 2) + reg, F32),
-                        VM((2, 8, 2) + reg, F32), VM((cols, cols), F32)],
+                        VM((2, 8, 2) + reg, F32), VM(reg, F32)],
         name="model",
     )(state.reshape(members * rows, cols), qt.reshape(-1, cols), qb.reshape(-1, cols),
       fields.reshape(-1, cols), ft.reshape(-1, cols), fb.reshape(-1, cols), mid, top, bot,
       member_mode.reshape(1, members), theta.T, obs_index)
-    return out.reshape(members, rows, cols), obs, thp
-
-
-def sums_kernel(n_gx, n_gy, n_ens, reduce_here, obs_ref, thp_ref, val_ref, sig_ref, full_ref, th_ref,
-                obs_all, part, rs, ens_send, ens_recv, rs_send, rs_recv, ag_send, ag_recv):
+    return out.reshape(members, rows, cols), obs
+
+
+def sums_kernel(n_gx, n_gy, n_ens, reduce_here, obs_ref, theta_ref, val_ref, sig_ref, full_ref, c_ref, th_ref,
+                obs_all, part, rs, c_own, cs, ens_send, ens_recv, rs_send, rs_recv, cs_send, cs_recv, ag_send, ag_recv):
     gx, gy, ens = lax.axis_index("gx"), lax.axis_index("gy"), lax.axis_index("ens")
     members = obs_ref.shape[0]
     n = n_gx * n_gy
@@ -406,35 +412,41 @@
                                             device_id=dev, device_id_type=MESH)
 
     mine = pl.ds(pl.multiple_of(ens * members, members), members)
-    copies = []
+    obs_copies, th_copies = [], []
     for k, p in enumerate(others):
-        copies.append(rdma(obs_ref, obs_all.at[mine], ens_send.at[2 * k], ens_recv.at[2 * k], {"ens": p}))
-        copies.append(rdma(thp_ref, th_ref.at[mine], ens_send.at[2 * k + 1], ens_recv.at[2 * k + 1], {"ens": p}))
-    for c in copies:
+        obs_copies.append(rdma(obs_ref, obs_all.at[mine], ens_send.at[2 * k], ens_recv.at[2 * k], {"ens": p}))
+        th_copies.append(rdma(theta_ref, th_ref.at[ens], ens_send.at[2 * k + 1], ens_recv.at[2 * k + 1], {"ens": p}))
+    for c in obs_copies + th_copies:
         c.start()
     obs_all[mine, :] = obs_ref[...]
-    th_ref[mine, :] = thp_ref[...]
-    for c in copies:
+    th_ref[ens] = theta_ref[...]
+    for c in obs_copies:
         c.wait()
 
     x = obs_all[...]
     mean = jnp.mean(x, axis=0, keepdims=True)
     inv = 1.0 / sig_ref[0]
     anom = (x - mean) * inv
-    d = jnp.broadcast_to((val_ref[0] - mean) * inv, x.shape)
+    d = jnp.broadcast_to((val_ref[0] - mean) * inv, (8, x.shape[1]))
     nt = (((1,), (1,)), ((), ()))
     total = x.shape[0]
-    part[:, 0:total] = lax.dot_general(anom, anom, nt, preferred_element_type=F32, precision=HIGH)
-    part[:, total:] = lax.dot_general(anom, d, nt, preferred_element_type=F32, precision=HIGH)
+    c_part = lax.dot_general(d, anom, nt, preferred_element_type=F32, precision=HIGH)[0:1]
+    gram = lax.dot_general(anom, anom, nt, preferred_element_type=F32, precision=HIGH)
 
     if not reduce_here:
-        full_ref[...] = part[...]
+        full_ref[...] = gram
+        c_ref[...] = c_part
+        for c in th_copies:
+            c.wait()
         return
+    c_own[...] = c_part
+    part[...] = gram
     own = total // n
     at = lambda p: pl.ds(pl.multiple_of(p * own, own), own)
     sends = [rdma(part.at[at(p)], rs.at[k], rs_send.at[k], rs_recv.at[k], w)
              for k, (p, w) in enumerate(zip(peers, where))]
-    for c in sends:
+    c_sends = [rdma(c_own, cs.at[k], cs_send.at[k], cs_recv.at[k], w) for k, w in enumerate(where)]
+    for c in sends + c_sends:
         c.start()
     acc = part[at(me), :]
     for k, c in enumerate(sends):
@@ -445,13 +457,18 @@
                for k, w in enumerate(where)]
     for c in gathers:
         c.start()
-    for c in sends:
+    acc = c_own[...]
+    for k, c in enumerate(c_sends):
+        c.wait_recv()
+        acc = acc + cs[k]
+    c_ref[...] = acc
+    for c in sends + c_sends:
         c.wait_send()
-    for c in gathers:
+    for c in th_copies + gathers:
         c.wait()
 
 
-def ensemble_sums(mesh, obs, thp, values, sigma):
+def ensemble_sums(mesh, obs, theta, values, sigma):
     n_gx, n_gy, n_ens = mesh.shape["gx"], mesh.shape["gy"], mesh.shape["ens"]
     members, cols = obs.shape
     total = members * n_ens
@@ -459,82 +476,110 @@
     reduce_here = total % (8 * n) == 0
     own = total // n if reduce_here else 8
     slots = n - 1 if reduce_here else 1
-    full, th = pl.pallas_call(
+    sds = jax.ShapeDtypeStruct
+    full, c, th = pl.pallas_call(
         functools.partial(sums_kernel, n_gx, n_gy, n_ens, reduce_here),
-        out_shape=[jax.ShapeDtypeStruct((total, 2 * total), F32), jax.ShapeDtypeStruct((total, cols), F32)],
+        out_shape=[sds((total, total), F32), sds((1, total), F32), sds((n_ens,) + theta.shape[::-1], F32)],
         in_specs=[vspec()] * 4,
-        out_specs=[vspec()] * 2,
-        scratch_shapes=[VM((total, cols), F32), VM((total, 2 * total), F32), VM((slots, own, 2 * total), F32)]
+        out_specs=[vspec()] * 3,
+        scratch_shapes=[VM((total, cols), F32), VM((total, total), F32), VM((slots, own, total), F32),
+                        VM((1, total), F32), VM((slots, 1, total), F32)]
         + [pltpu.SemaphoreType.DMA((2 * (n_ens - 1),))] * 2
-        + [pltpu.SemaphoreType.DMA((slots,))] * 4,
+        + [pltpu.SemaphoreType.DMA((slots,))] * 6,
         compiler_params=pltpu.CompilerParams(collective_id=1, has_side_effects=True),
         name="sums",
-    )(obs, thp, values, sigma)
+    )(obs, theta.T, values, sigma)
     if not reduce_here:
-        full = lax.psum(full, ("gx", "gy"))
-    return full, th
-
-
-def solve_kernel(members, full_ref, th_ref, out_ref, xs):
+        full, c = lax.psum((full, c), ("gx", "gy"))
+    return full, c, th
+
+
+def solve_kernel(members, full_ref, c_ref, th_ref, out_ref, xs):
     total = full_ref.shape[0]
     blocks = total // 8
+    n_ens, params = th_ref.shape[0], th_ref.shape[1]
     shape = (8, total)
     lane = lax.broadcasted_iota(jnp.int32, shape, 1)
     sub = lax.broadcasted_iota(jnp.int32, shape, 0)
-    th = th_ref[...]
-    mean = jnp.mean(th, axis=0, keepdims=True)
+    tht = jnp.concatenate([th_ref[e] for e in range(n_ens)], axis=1)
+    spread = tht - jnp.mean(tht, axis=1, keepdims=True)
+    xs[...] = jnp.zeros_like(xs)
+    xs[0:params, :] = spread
+    cols_of = xs[...].T
     A, R = [], []
     for k in range(blocks):
         rows = slice(8 * k, 8 * k + 8)
-        A.append(full_ref[rows, 0:total] + jnp.where(lane == sub + 8 * k, float(total - 1), 0.0))
-        R.append(th[rows] - mean)
+        A.append(full_ref[rows, :] + jnp.where(lane == sub + 8 * k, float(total - 1), 0.0))
+        R.append(cols_of[rows])
+
+    def splat(x):
+        return jnp.broadcast_to(x, shape)
+
     for k in range(blocks):
-        pa, pr = A[k], R[k]
+        rs_, rr = [], []
+        d = {}
         for j in range(8):
-            c = pa[:, 8 * k + j:8 * k + j + 1]
-            inv = 1.0 / c[j:j + 1]
-            na, nr = pa[j:j + 1] * inv, pr[j:j + 1] * inv
-            pa = jnp.where(sub == j, na, pa - c * na)
-            pr = jnp.where(sub == j, nr, pr - c * nr)
-        A[k], R[k] = pa, pr
+            row = splat(A[k][j:j + 1])
+            rs_.append(row)
+            rr.append(splat(R[k][j:j + 1]))
+            for i in range(j, 8):
+                d[j, i] = splat(row[:, 8 * k + i:8 * k + i + 1])
+        inv = []
+        for j in range(8):
+            inv.append(1.0 / d[j, j])
+            for i in range(j + 1, 8):
+                m = d[j, i] * inv[j]
+                rs_[i] = rs_[i] - m * rs_[j]
+                rr[i] = rr[i] - m * rr[j]
+                for q in range(i, 8):
+                    d[i, q] = d[i, q] - m * d[j, q]
+        for i in reversed(range(8)):
+            for j in range(i + 1, 8):
+                rs_[i] = rs_[i] - d[i, j] * rs_[j]
+                rr[i] = rr[i] - d[i, j] * rr[j]
+            rs_[i] = rs_[i] * inv[i]
+            rr[i] = rr[i] * inv[i]
+        a, r = rs_[7], rr[7]
+        for j in range(7):
+            a = jnp.where(sub == j, rs_[j], a)
+            r = jnp.where(sub == j, rr[j], r)
+        A[k], R[k] = a, r
         for i in list(range(k + 1, blocks)) + list(range(k)):
             a, r = A[i], R[i]
             for j in range(8):
-                c = A[i][:, 8 * k + j:8 * k + j + 1]
-                a = a - c * pa[j:j + 1]
-                r = r - c * pr[j:j + 1]
+                c = splat(A[i][:, 8 * k + j:8 * k + j + 1])
+                if k + 1 < blocks:
+                    a = a - c * rs_[j]
+                r = r - c * rr[j]
             A[i], R[i] = a, r
-    shift = jnp.zeros((1, th.shape[1]), F32)
     for k in range(blocks):
-        rows = slice(8 * k, 8 * k + 8)
-        shift = shift + jnp.sum(full_ref[rows, total:] * R[k], axis=0, keepdims=True)
-        xs[rows, :] = R[k]
+        xs[8 * k:8 * k + 8, :] = R[k]
+    x = xs[...].T[0:8]
+    shift = jnp.sum(x * c_ref[...], axis=1, keepdims=True)
+    new = (jnp.mean(tht, axis=1, keepdims=True) + shift[0:params]) + float(total - 1) * x[0:params]
     ens = lax.axis_index("ens")
-    x = xs[pl.ds(pl.multiple_of(ens * members, members), members), :]
-    new = mean + shift + float(total - 1) * x
-    xs[0:members, :] = new
-    out_ref[...] = xs[...].T[0:out_ref.shape[0], 0:members]
-
-
-def solve(full, th, theta):
+    for e in range(n_ens):
+        @pl.when(ens == e)
+        def _():
+            out_ref[...] = new[:, e * members:(e + 1) * members]
+
+
+def solve(full, c, th, theta):
     return pl.pallas_call(
         functools.partial(solve_kernel, theta.shape[0]),
         out_shape=jax.ShapeDtypeStruct(theta.shape[::-1], F32),
-        in_specs=[vspec()] * 2,
+        in_specs=[vspec()] * 3,
         out_specs=vspec(),
-        scratch_shapes=[VM(th.shape, F32)],
+        scratch_shapes=[VM(full.shape, F32)],
         name="solve",
-    )(full, th).T
+    )(full, c, th).T
 
 
 def local(mesh, state, u_vel, v_vel, land, forcing, member_mode, theta, obs_index, obs_values, obs_sigma):
-    ocean = (1 - land).astype(F32)
-    rows, cols = u_vel.shape
-    fields = jnp.concatenate([forcing, u_vel[None], v_vel[None], ocean[None], jnp.zeros((5, rows, cols), F32)], 0)
-    halos = halo_exchange(mesh, state, fields)
-    final, obs, thp = run_model(mesh, state, fields, halos, member_mode, theta, obs_index)
-    full, th = ensemble_sums(mesh, obs, thp, obs_values, obs_sigma)
-    return final, solve(full, th, theta)
+    fields, *halos = halo_exchange(mesh, state, forcing, u_vel, v_vel, land)
+    final, obs = run_model(mesh, state, fields, halos, member_mode, theta, obs_index)
+    full, c, th = ensemble_sums(mesh, obs, theta, obs_values, obs_sigma)
+    return final, solve(full, c, th, theta)
 
 
 def solution(mesh):

time: 67.9 us -> 57.5 us (0.85)
  Pallas kernels: 63.9 us -> 56.6 us
  local copies, waits for them, and re-layouts: 2.88 us -> 0 us
    pallas_call x1, Pallas kernels: 12.1 us -> 6.18 us  [solve(): pl.pallas_call(functools.partial(solve_kernel, theta.shape[0]), out_shape...]
    unnamed x11 -> x0, local copies, waits for them, and re-layouts: 2.88 us -> none
    pallas_call x1, Pallas kernels: 22 us -> 20.3 us  [ensemble_sums(): pl.pallas_call(functools.partial(sums_kernel, n_gx, n_gy, n_ens, reduce_h...]
where the time goes in v3:
time: 57.5 us; the launch traced here: 57.2 us
  Pallas kernels  56.6 us (98%)
  between operations  0.65 us (1%)
    pallas_call x1, Pallas kernels, ensemble_sums(): pl.pallas_call(functools.partial(sums_kernel, n_gx, n_gy, n_ens, reduce_h...  20.3 us
    pallas_call x1, Pallas kernels, run_model(): pl.pallas_call(functools.partial(model_kernel, mesh.shape['gy']), out_sha...  17.7 us
    pallas_call x1, Pallas kernels, halo_exchange(): pl.pallas_call(functools.partial(halo_kernel, mesh.shape['gx'], mesh.shap...  12.3 us
    pallas_call x1, Pallas kernels, solve(): pl.pallas_call(functools.partial(solve_kernel, theta.shape[0]), out_shape...  6.18 us

profile of v3, /device:TPU:0, one launch (start us, length us, event | category | flops | bytes accessed | tf_op | source)
XLA Modules:
  0.0 57.2 jit_solution(11697544359002553169)
XLA Ops:
  0.6 12.3 %halo.1 = (f32[16,16,128]{2,1,0:T(8,128)}, f32[64,8,128]{2,1,0:T(8,128)}, f32[64,8,128]{2,1,0:T(8,128)}, f32[16,8,128]{2,1,0:T(8,128)}, f32[16,8,128]{2,1,0:T(8,...) custom-call(f32[64,16,128]{2,1,0:T(8,128)} %q_ref.1, f32[8,16,128]{2,1,0:T(8,128)} %forcing_ref.1, ...), custom_call_target="tpu_custom_call" | custom-call | tf_op jit(solution)/shard_map/halo/pallas_call | solution.py:125
  12.9 17.7 %model.1 = (f32[1024,128]{1,0:T(8,128)}, f32[64,128]{1,0:T(8,128)}) custom-call(f32[1024,128]{1,0:T(8,128)} %bitcast.10, f32[512,128]{1,0:T(8,128)} %bitcast.11, f32[512,128]{1,0:T(8,128)} %bitcast.12, f32[256,128]{1,0:T(8,128)} %bitcast.13, f32[128,128]{1,0:T(8,128)} %bitcast.14, f32[128,128]{1,0:T(8,128)} %bitcast.15, ...), custom_call_target="tpu_custom_call" | custom-call | tf_op jit(solution)/shard_map/model/pallas_call | solution.py:377
  30.7 20.3 %sums.1 = (f32[128,128]{1,0:T(8,128)}, f32[1,128]{1,0:T(1,128)}, f32[2,4,64]{2,1,0:T(4,128)}) custom-call(f32[64,128]{1,0:T(8,128)} %get-tuple-element.24.obs_ref, f32[4,64]{1,0:T(4,128)} %bitcast.17, f32[1,1,128]{2,1,0:T(1,128)} %val_ref.1, f32[1,1,128]{2,1,0:T(1,128)} %sig_ref.1), custom_call_target="tpu_custom_call" | custom-call | tf_op jit(solution)/shard_map/sums/pallas_call | solution.py:480
  51.0 6.2 %solve.1 = f32[4,64]{1,0:T(4,128)} custom-call(f32[128,128]{1,0:T(8,128)} %get-tuple-element.25.full_ref, f32[1,128]{1,0:T(1,128)} %get-tuple-element.26.c_ref, f32[2,4,64]{2,1,0:T(4,128)} %get-tuple-element.27.th_ref), custom_call_target="tpu_custom_call" | custom-call | tf_op jit(solution)/shard_map/solve/pallas_call | solution.py:568

commit v4 on v3

--- a/solution.py
+++ b/solution.py
@@ -222,21 +222,22 @@
             for c in range(8):
                 H[0, side, c, half] = ys[c]
 
-    for i in range(n_rows):
-        if i < DEPTH:
-            ref, per, k, fr = qt_ref, DEPTH, i, ft_ref
-        elif i < DEPTH + rows:
-            ref, per, k, fr = q_ref, rows, i - DEPTH, f_ref
-        else:
-            ref, per, k, fr = qb_ref, DEPTH, i - DEPTH - rows, fb_ref
-        ys = butterfly([masked(i, ref[pl.ds(v * per + k, 8, stride=8 * per), :]) for v in range(8)])
-        for c in range(8):
-            Q[0, i, c] = ys[c]
-        if 2 <= i < n_rows - 2:
-            x = masked(i, fr[pl.ds(k, 8, stride=per), :])
-            ys = butterfly([gather(x, modes[v], 0) for v in range(8)])
-            for c in range(8):
-                FO[i, c] = gain * ys[c]
+    def enter(ref, per, fr, base, ok):
+        def body(k, carry):
+            def keep_in(x):
+                return x if ok is None else jnp.where(ok, x, 0.0)
+            ys = butterfly([keep_in(ref[pl.ds(v * per + k, 8, stride=8 * per), :]) for v in range(8)])
+            x = keep_in(fr[pl.ds(k, 8, stride=per), :])
+            zs = butterfly([gather(x, modes[v], 0) for v in range(8)])
+            for c in range(8):
+                Q[0, base + k, c] = ys[c]
+                FO[base + k, c] = gain * zs[c]
+            return carry
+        lax.fori_loop(0, per, body, 0)
+
+    enter(qt_ref, DEPTH, ft_ref, 0, has_up)
+    enter(q_ref, rows, f_ref, DEPTH, None)
+    enter(qb_ref, DEPTH, fb_ref, DEPTH + rows, has_down)
 
     first, last = lane < 8, lane >= cols - 8
 

time: 57.5 us -> 55.8 us (0.970)
  Pallas kernels: 56.6 us -> 54.9 us
    pallas_call x1, Pallas kernels: 17.7 us -> 16.1 us  [run_model(): pl.pallas_call(functools.partial(model_kernel, mesh.shape['gy']), out_sha...]
where the time goes in v4:
time: 55.8 us; the launch traced here: 55.5 us
  Pallas kernels  54.9 us (98%)
  between operations  0.65 us (1%)
    pallas_call x1, Pallas kernels, ensemble_sums(): pl.pallas_call(functools.partial(sums_kernel, n_gx, n_gy, n_ens, reduce_h...  20.3 us
    pallas_call x1, Pallas kernels, run_model(): pl.pallas_call(functools.partial(model_kernel, mesh.shape['gy']), out_sha...  16.1 us
    pallas_call x1, Pallas kernels, halo_exchange(): pl.pallas_call(functools.partial(halo_kernel, mesh.shape['gx'], mesh.shap...  12.3 us
    pallas_call x1, Pallas kernels, solve(): pl.pallas_call(functools.partial(solve_kernel, theta.shape[0]), out_shape...  6.18 us

profile of v4, /device:TPU:0, one launch (start us, length us, event | category | flops | bytes accessed | tf_op | source)
XLA Modules:
  0.0 55.5 jit_solution(6070237614134999758)
XLA Ops:
  0.6 12.3 %halo.1 = (f32[16,16,128]{2,1,0:T(8,128)}, f32[64,8,128]{2,1,0:T(8,128)}, f32[64,8,128]{2,1,0:T(8,128)}, f32[16,8,128]{2,1,0:T(8,128)}, f32[16,8,128]{2,1,0:T(8,...) custom-call(f32[64,16,128]{2,1,0:T(8,128)} %q_ref.1, f32[8,16,128]{2,1,0:T(8,128)} %forcing_ref.1, ...), custom_call_target="tpu_custom_call" | custom-call | tf_op jit(solution)/shard_map/halo/pallas_call | solution.py:125
  12.9 16.1 %model.1 = (f32[1024,128]{1,0:T(8,128)}, f32[64,128]{1,0:T(8,128)}) custom-call(f32[1024,128]{1,0:T(8,128)} %bitcast.10, f32[512,128]{1,0:T(8,128)} %bitcast.11, f32[512,128]{1,0:T(8,128)} %bitcast.12, f32[256,128]{1,0:T(8,128)} %bitcast.13, f32[128,128]{1,0:T(8,128)} %bitcast.14, f32[128,128]{1,0:T(8,128)} %bitcast.15, ...), custom_call_target="tpu_custom_call" | custom-call | tf_op jit(solution)/shard_map/model/pallas_call | solution.py:378
  29.0 20.3 %sums.1 = (f32[128,128]{1,0:T(8,128)}, f32[1,128]{1,0:T(1,128)}, f32[2,4,64]{2,1,0:T(4,128)}) custom-call(f32[64,128]{1,0:T(8,128)} %get-tuple-element.24.obs_ref, f32[4,64]{1,0:T(4,128)} %bitcast.17, f32[1,1,128]{2,1,0:T(1,128)} %val_ref.1, f32[1,1,128]{2,1,0:T(1,128)} %sig_ref.1), custom_call_target="tpu_custom_call" | custom-call | tf_op jit(solution)/shard_map/sums/pallas_call | solution.py:481
  49.3 6.2 %solve.1 = f32[4,64]{1,0:T(4,128)} custom-call(f32[128,128]{1,0:T(8,128)} %get-tuple-element.25.full_ref, f32[1,128]{1,0:T(1,128)} %get-tuple-element.26.c_ref, f32[2,4,64]{2,1,0:T(4,128)} %get-tuple-element.27.th_ref), custom_call_target="tpu_custom_call" | custom-call | tf_op jit(solution)/shard_map/solve/pallas_call | solution.py:569
